TPU v7x, 256 devices: a whole 4x4x8 slice. The times are simulated.
256 devices in a mesh: dp: 128 (over z, y_lo, x, core), mp: 2 (over y_hi).
Axes of the slice: x: 4, y: 4 (y_hi: 2, y_lo: 2; y = y_hi * 2 + y_lo), z: 8, core: 2. Of those that a mesh axis runs over, the one named last changes fastest.
Arguments:
- context: bfloat16 [40960, 2048], P('dp', 'mp'), may hold values from -24 to 24
- out_weight: bfloat16 [2048, 3584], P('mp'), may hold values from -0.125 to 0.125
- cotangent: bfloat16 [40960, 3584], P('dp'), may hold values from -0.059814453 to 0.059814453
- norm_gain: float32 [3584], replicated, may hold values from 0.5 to 1.5
- first_moment: float32 [2, 1024, 3584], P('mp', 'dp'), may hold values from -6 to 6
- second_moment: float32 [2, 1024, 3584], P('mp', 'dp'), may hold values from 0.01 to 1
Outputs:
- new_weight: bfloat16 [2, 1024, 3584], P('mp', 'dp')
- new_first: float32 [2, 1024, 3584], P('mp', 'dp')
- new_second: float32 [2, 1024, 3584], P('mp', 'dp')
- grad_gain: float32 [3584], replicated
- grad_context: bfloat16 [40960, 2048], P('dp', 'mp')
All inputs are finite; a program needn't handle non-finite values.
Results may differ from a plain program's by a relative error of at most 0.005.
Values may be sent and summed in bfloat16 or wider, within the bound.
A program may use at most 128 MiB of HBM per device.

v0:
```python
import jax
import jax.numpy as jnp
from jax import lax
from jax.sharding import Mesh
from jax.sharding import PartitionSpec as P

DP = ("dp_0", "dp_1", "dp_2", "dp_3")


norm_floor = 0.1
learn_rate = 0.01
beta_one = 0.9
beta_two = 0.95
adam_floor = 1e-08


def split_up(shard, dim, devices):
    before, after = (shard.shape[:dim], shard.shape[dim + 1 :])
    return jnp.moveaxis(shard.reshape(*before, devices, -1, *after), dim, 0)


def sent_and_summed(shard, axis, dim):
    tiles = split_up(shard, dim, lax.axis_size(axis))
    arrived = lax.all_to_all(tiles, axis, split_axis=0, concat_axis=0, tiled=True)
    return arrived.astype(jnp.float32).sum(axis=0)


def copy_for_each(shard, axis):
    copies = jnp.broadcast_to(shard, (lax.axis_size(axis), *shard.shape))
    return lax.all_to_all(copies, axis, split_axis=0, concat_axis=0, tiled=True)


def taken_together(shard, axis):
    return copy_for_each(shard, axis).sum(axis=0)


def joined_along(tiles, dim):
    lengths = list(tiles.shape[1:])
    lengths[dim] *= tiles.shape[0]
    return jnp.moveaxis(tiles, 0, dim).reshape(lengths)


def collect(shard, axis, dim):
    return joined_along(copy_for_each(shard, axis), dim)


def by_axis(shard, axes):
    for axis in axes:
        shard = lax.psum(shard, axis)
    return shard


def sum_by_chip_2(shard, chips, core, dim):
    sizes = (lax.axis_size(chips), lax.axis_size(core))
    tiles = split_up(shard, dim, sizes[0] * sizes[1])
    inside = tiles.shape[1:]
    tiles = tiles.reshape(*sizes, *inside).swapaxes(0, 1).reshape(-1, *inside)
    tiles = lax.psum_scatter(tiles, core, scatter_dimension=0, tiled=True)
    return lax.psum_scatter(tiles, chips, scatter_dimension=0, tiled=True)[0]


def adam_update(master, first_moment, second_moment, grad_shard):
    new_first = beta_one * first_moment + (1.0 - beta_one) * grad_shard
    new_second = beta_two * second_moment + (1.0 - beta_two) * grad_shard * grad_shard
    new_weight = (master - learn_rate * new_first / (jnp.sqrt(new_second) + adam_floor)).astype(
        jnp.bfloat16
    )
    return (new_weight, new_first, new_second)


def per_device(context, out_weight, cotangent, norm_gain, first_moment, second_moment):
    width = out_weight.shape[1]
    partial_value = jnp.dot(context, out_weight, preferred_element_type=jnp.float32)
    half_width = width // lax.axis_size("mp")
    offset = lax.axis_index("mp") * half_width
    attn_half = sent_and_summed(partial_value.astype(jnp.bfloat16), "mp", 1)
    gain_half = lax.dynamic_slice_in_dim(norm_gain, offset, half_width, 0)
    upstream = lax.dynamic_slice_in_dim(cotangent, offset, half_width, 1).astype(jnp.float32)
    squares = jnp.sum(attn_half * attn_half, axis=-1, keepdims=True)
    total_sq = taken_together(squares, "mp")
    inverse = lax.rsqrt(total_sq / width + norm_floor)
    normed = attn_half * inverse
    scaled = upstream * gain_half
    product_half = jnp.sum(scaled * normed, axis=-1, keepdims=True)
    product_all = lax.psum(product_half, "mp")
    grad_half = (inverse * (scaled - normed * (product_all / width))).astype(jnp.bfloat16)
    grad_attn = collect(grad_half, "mp", 1)
    gain_part = jnp.sum(upstream * normed, axis=0)
    gain_total = by_axis(gain_part, DP)
    grad_gain = lax.all_gather(gain_total, "mp", axis=0, tiled=True)
    shard_rows = first_moment.shape[1]
    master = lax.dynamic_slice_in_dim(
        out_weight, lax.axis_index(DP) * shard_rows, shard_rows, 0
    ).astype(jnp.float32)[None]
    grad_shard = sum_by_chip_2(
        lax.dot_general(
            context, grad_attn, (((0,), (0,)), ((), ())), preferred_element_type=jnp.float32
        ),
        ("dp_0", "dp_1", "dp_2"),
        "dp_3",
        0,
    )
    grad_context = lax.dot_general(
        grad_attn, out_weight, (((1,), (1,)), ((), ())), preferred_element_type=jnp.float32
    ).astype(jnp.bfloat16)
    new_weight, new_first, new_second = adam_update(
        master, first_moment, second_moment, grad_shard[None]
    )
    return (new_weight, new_first, new_second, grad_gain, grad_context)


def solution(mesh):
    finer = Mesh(
        mesh.devices.reshape(8, 2, 4, 2, mesh.shape["mp"]), ("dp_0", "dp_1", "dp_2", "dp_3", "mp")
    )
    placed = (P(DP, "mp"), P("mp", None), P(DP, None), P(), P("mp", DP, None), P("mp", DP, None))
    return jax.shard_map(
        per_device,
        mesh=finer,
        in_specs=placed,
        out_specs=(P("mp", DP, None), P("mp", DP, None), P("mp", DP, None), P(), P(DP, "mp")),
        check_vma=False,
    )
```

profile of v0, /device:TPU:16, one launch (start us, length us, event | category | flops | bytes accessed | tf_op | source)
XLA Modules:
  0.0 488.8 jit_solution(13827067730248141834)
XLA Ops:
  7.2 0.0 copy-start
  7.2 1.1 copy-done
  8.3 5.6 %convolution_convert_fusion = bf16[320,3584]{1,0:T(8,128)(2,1)S(1)} fusion(bf16[320,1024]{1,0:T(8,128)(2,1)S(1)} %copy-done, bf16[1024,3584]{1,0:T(8,128)(2,1)} %param.7), kind=kOutput, calls=%fused_computation | convolution fusion | flops 2349957120 | bytes 10289152 | tf_op jit(solution)/shard_map/dot_general | solution.py:73
  13.9 0.1 copy.19
  14.0 29.8 %all_to_all.15 = bf16[2,320,1792]{2,1,0:T(8,128)(2,1)S(1)} all-to-all(bf16[2,320,1792]{2,1,0:T(8,128)(2,1)S(1)} %bitcast.29), channel_id=1, replica_groups=mesh['dp_0'=8,'dp_1'=2,'dp_2'=4,'dp_3'=2,'mp'=2] {'mp'}, dimensions={0} | all-to-all | bytes 4587520 | tf_op jit(solution)/shard_map/all_to_all | solution.py:24
  43.8 0.4 convert_reduce_fusion
  44.2 0.0 copy-start.3
  44.2 0.2 multiply_reduce_fusion
  44.5 0.6 broadcast_in_dim.19
  45.0 6.5 %all-to-all-start.1 = ((f32[2,320,1]{1,2,0:T(1,128)}), f32[2,320,1]{1,2,0:T(1,128)S(1)}, u32[]{:S(2)}, u32[]{:S(2)}) async-start(f32[2,320,1]{1,2,0:T(1,128)} %broadcast_in_dim.19), calls=%async_computation.1 | async-start | bytes 6144 | tf_op jit(solution)/shard_map/all_to_all | solution.py:30
  51.5 0.0 reduce-scatter.3.cloned.1.call-start
  51.5 0.0 copy-done.3
  51.5 0.1 dynamic_slice.11
  51.6 1.7 all-to-all-done.1
  53.3 2.1 fusion.5
  55.4 6.4 %psum.35 = f32[320,1]{0,1:T(1,128)S(1)} all-reduce(f32[320,1]{0,1:T(1,128)S(1)} %broadcast_in_dim.20), channel_id=1, replica_groups=mesh['dp_0'=8,'dp_1'=2,'dp_2'=4,'dp_3'=2,'mp'=2] {'mp'}, use_global_device_ids=true, to_apply=%region_4.0 | all-reduce | flops 320 | bytes 2560 | tf_op jit(solution)/shard_map/psum | solution.py:85
  61.9 1.8 fusion.4
  63.7 0.1 broadcast_in_dim.21
  63.9 28.1 %all_to_all.16 = bf16[2,320,1792]{2,1,0:T(8,128)(2,1)S(1)} all-to-all(bf16[2,320,1792]{2,1,0:T(8,128)(2,1)S(1)} %broadcast_in_dim.21), channel_id=1, replica_groups=mesh['dp_0'=8,'dp_1'=2,'dp_2'=4,'dp_3'=2,'mp'=2] {'mp'}, dimensions={0} | all-to-all | bytes 4587520 | tf_op jit(solution)/shard_map/all_to_all | solution.py:30
  92.0 0.2 copy.17
  92.2 7.3 %fusion.9 = f32[3584,1024]{0,1:T(8,128)} fusion(bf16[320,3584]{1,0:T(8,128)(2,1)S(1)} %bitcast.27, bf16[320,1024]{1,0:T(8,128)(2,1)S(1)} %copy-done), kind=kOutput, calls=%fused_computation.20 | convolution fusion | flops 2348810240 | bytes 17629184 | tf_op jit(solution)/shard_map/dot_general | solution.py:96
  99.5 11.6 %copy.15 = f32[2,64,8,3584]{3,2,1,0:T(8,128)} copy(f32[2,64,8,3584]{3,2,0,1:T(8,128)} %bitcast.26) | data formatting | bytes 29360128 | tf_op jit(solution)/shard_map/transpose | solution.py:57
  111.1 0.0 reduce-scatter.3.cloned.1.call-update
  111.1 0.0 reduce-scatter.5.cloned.1.call-start
  111.1 33.6 %reduce-scatter.3.cloned.1.call-done = f32[64,8,3584]{2,1,0:T(8,128)} async-done(((f32[128,8,3584]{2,1,0:T(8,128)}), f32[64,8,3584]{2,1,0:T(8,128)}) %reduce-scatter.3.cloned.1.call-update) | async-done | bytes 7340048 | tf_op jit(solution)/shard_map/reduce_scatter | solution.py:58
  144.7 0.0 reduce-scatter.5.cloned.1.call-update
  144.7 17.7 %psum.36 = f32[1792]{0:T(1024)S(1)} all-reduce(f32[1792]{0:T(1024)S(1)} %get-tuple-element.5), channel_id=1, replica_groups=mesh['dp_0'=8,'dp_1'=2,'dp_2'=4,'dp_3'=2,'mp'=2] {'dp_0'}, use_global_device_ids=true, to_apply=%region_8.0 | all-reduce | flops 1792 | bytes 14336 | tf_op jit(solution)/shard_map/psum | solution.py:49
  162.5 5.0 %psum.37 = f32[1792]{0:T(1024)S(1)} all-reduce(f32[1792]{0:T(1024)S(1)} %psum.36), channel_id=1, replica_groups=mesh['dp_0'=8,'dp_1'=2,'dp_2'=4,'dp_3'=2,'mp'=2] {'dp_1'}, use_global_device_ids=true, to_apply=%region_9.0 | all-reduce | flops 1792 | bytes 14336 | tf_op jit(solution)/shard_map/psum | solution.py:49
  167.5 11.2 %psum.38 = f32[1792]{0:T(1024)S(1)} all-reduce(f32[1792]{0:T(1024)S(1)} %psum.37), channel_id=1, replica_groups=mesh['dp_0'=8,'dp_1'=2,'dp_2'=4,'dp_3'=2,'mp'=2] {'dp_2'}, use_global_device_ids=true, to_apply=%region_10.0 | all-reduce | flops 1792 | bytes 14336 | tf_op jit(solution)/shard_map/psum | solution.py:49
  178.7 2.5 psum.39
  181.2 5.9 %all-gather = f32[2,1,1792]{2,1,0:T(1,128)S(1)} all-gather(f32[1,1,1792]{2,1,0:T(1,128)S(1)} %reshape.33), channel_id=1, replica_groups=mesh['dp_0'=8,'dp_1'=2,'dp_2'=4,'dp_3'=2,'mp'=2] {'mp'}, dimensions={0}, use_global_device_ids=true | all-gather | bytes 21504 | tf_op jit(solution)/shard_map/all_gather | solution.py:90
  187.2 0.6 reshape.34
  187.8 0.0 copy-start.1
  187.8 0.0 copy-start.2
  187.8 6.6 %convolution_convert_fusion.1 = bf16[320,1024]{1,0:T(8,128)(2,1)} fusion(bf16[320,3584]{1,0:T(8,128)(2,1)S(1)} %bitcast.28, bf16[1024,3584]{1,0:T(8,128)(2,1)} %param.7), kind=kOutput, calls=%fused_computation.12 | convolution fusion | flops 2349137920 | bytes 10289152 | tf_op jit(solution)/shard_map/dot_general | solution.py:103
  194.3 286.0 %reduce-scatter.5.cloned.1.call-done = f32[1,8,3584]{2,1,0:T(8,128)} async-done(((f32[64,8,3584]{2,1,0:T(8,128)}), f32[1,8,3584]{2,1,0:T(8,128)}) %reduce-scatter.5.cloned.1.call-update) | async-done | bytes 114704 | tf_op jit(solution)/shard_map/reduce_scatter | solution.py:59
  480.3 0.0 copy-done.1
  480.3 0.0 copy-done.2
  480.3 1.7 fusion.7
  (6 shorter events, 0.1 us)
Async XLA Ops:
  7.2 1.1 copy-start
  44.2 7.3 %copy-start.3 = (f32[3584]{0:T(1024)S(1)}, f32[3584]{0:T(1024)}, u32[]{:S(2)}) copy-start(f32[3584]{0:T(1024)} %param.9) | copy-start | bytes 43012
  45.0 8.2 %all-to-all-start.1 = ((f32[2,320,1]{1,2,0:T(1,128)}), f32[2,320,1]{1,2,0:T(1,128)S(1)}, u32[]{:S(2)}, u32[]{:S(2)}) async-start(f32[2,320,1]{1,2,0:T(1,128)} %broadcast_in_dim.19), calls=%async_computation.1 | async-start | bytes 6144 | tf_op jit(solution)/shard_map/all_to_all | solution.py:30
  51.5 93.2 %reduce-scatter.3.cloned.1.call-start = ((), (), s32[]{:S(2)}) async-start(), calls=%async_computation.5 | async-start | bytes 22020096 | tf_op jit(solution)/shard_map/reduce_scatter | solution.py:58
  111.1 369.2 %reduce-scatter.5.cloned.1.call-start = ((), (), s32[]{:S(2)}) async-start(), calls=%async_computation.6 | async-start | bytes 7454720 | tf_op jit(solution)/shard_map/reduce_scatter | solution.py:59
  187.8 292.5 %copy-start.1 = (f32[1,8,3584]{2,1,0:T(8,128)S(1)}, f32[1,8,3584]{2,1,0:T(8,128)}, u32[]{:S(2)}) copy-start(f32[1,8,3584]{2,1,0:T(8,128)} %param.10) | copy-start | bytes 344068
  187.8 292.5 %copy-start.2 = (f32[1,8,3584]{2,1,0:T(8,128)S(1)}, f32[1,8,3584]{2,1,0:T(8,128)}, u32[]{:S(2)}) copy-start(f32[1,8,3584]{2,1,0:T(8,128)} %param.11) | copy-start | bytes 344068
Sparse Core Ops, SparseCore 0:
  111.2 33.4 reduce-scatter.2
  147.2 333.0 reduce-scatter.4
where the time goes:
time: 489 us
  waiting for transfers between devices  321 us (66%)
  blocking collectives  107 us (22%)
  matrix products  19.5 us (4%)
  local copies, waits for them, and re-layouts  14.4 us (3%)
  between operations  14.1 us (3%)
  starting transfers between devices  6.5 us (1%)
  other arithmetic  6.32 us (1%)
    reduce_scatter x1, waiting for transfers between devices, sum_by_chip_2(): return lax.psum_scatter(tiles, chips, scatter_dimension=0, tiled=True)[0]  286 us
    psum x4, blocking collectives, by_axis(): shard = lax.psum(shard, axis)  36.4 us
    reduce_scatter x1, waiting for transfers between devices, sum_by_chip_2(): tiles = lax.psum_scatter(tiles, core, scatter_dimension=0, tiled=True)  33.6 us
    all_to_all x1, blocking collectives, sent_and_summed(): lax.all_to_all(tiles, axis, split_axis=0, concat_axis=0, tiled=True)  29.8 us
    all_to_all x1, blocking collectives, copy_for_each(): return lax.all_to_all(copies, axis, split_axis=0, concat_axis=0, tiled=True)  28.1 us
    transpose x1, local copies, waits for them, and re-layouts, sum_by_chip_2(): tiles = tiles.reshape(*sizes, *inside).swapaxes(0, 1).reshape(-1, *inside)  11.6 us
  transfers between devices with their start and end apart: 3, of which 3 were waited for; matrix products, arithmetic and copies ran while one was open for 1% of the time, Pallas kernels for 0%

commit v1 on v0

v1 whole, which is shorter than its diff:
```python
import functools

import jax
import jax.numpy as jnp
from jax import lax
from jax.experimental import pallas as pl
from jax.experimental.pallas import tpu as pltpu
from jax.sharding import Mesh
from jax.sharding import PartitionSpec as P

DP = ("dp_0", "dp_1", "dp_2", "dp_3")
MESH = pl.DeviceIdType.MESH
F32 = jnp.float32
BF16 = jnp.bfloat16

norm_floor = 0.1
learn_rate = 0.01
beta_one = 0.9
beta_two = 0.95
adam_floor = 1e-08

QR = 256


def dot_nn(a, b):
    return lax.dot_general(a, b, (((1,), (0,)), ((), ())), preferred_element_type=F32)


def dot_tn(a, b):
    return lax.dot_general(a, b, (((0,), (0,)), ((), ())), preferred_element_type=F32)


def dot_nt(a, b):
    return lax.dot_general(a, b, (((1,), (1,)), ((), ())), preferred_element_type=F32)


def send(src, dst, send_sem, recv_sem, axis, peer):
    return pltpu.make_async_remote_copy(
        src_ref=src,
        dst_ref=dst,
        send_sem=send_sem,
        recv_sem=recv_sem,
        device_id={axis: peer},
        device_id_type=MESH,
    )


def kernel(
    dims,
    ctx_hbm, w_hbm, cot_hbm, gain_ref, m1_hbm, m2_hbm,
    nw_ref, n1_ref, n2_ref, gg_ref, gc_ref,
    ctx_o, ctx_s, wv, cot, att, psend, precv, ssr, spr, gaf, gas,
    grad, r1, r2, zs, zr, yt, yr, fs, gr, m1v, m2v, gz, gx, gy, gm, gk,
    ld_w, ld, c_sem, p_s, p_r, ga_s, ga_r, sa_s, sa_r, x1_s, x1_r, x2_s, x2_r,
    z_s, z_r, y_s, y_r, f_sem, gz_s, gz_r, gx_s, gx_r, gt_s, gt_r,
):
    NZ, NY, NX, TH, H, D, NB, CB = dims
    NB2 = 2 * NB
    ZY = NZ * NY
    HZ = ZY // 2
    T = 2 * TH
    z = lax.axis_index("dp_0")
    yl = lax.axis_index("dp_1")
    x = lax.axis_index("dp_2")
    c = lax.axis_index("dp_3")
    m = lax.axis_index("mp")

    def away(me, d, n):
        return lax.rem(me + d, n)

    right, left, across = away(x, 1, NX), away(x, NX - 1, NX), away(x, 2, NX)
    om, oc, oy = 1 - m, 1 - c, 1 - yl

    def each_block(n, body):
        def step(i, carry):
            body(i)
            return carry

        lax.fori_loop(0, n, step, 0)

    ctx_loads = [
        pltpu.make_async_copy(ctx_hbm.at[pl.ds(k * TH, TH), :], ctx_o.at[k], ld.at[k]) for k in range(2)
    ]
    cot_load = pltpu.make_async_copy(
        cot_hbm.at[pl.ds(pl.multiple_of(m * TH, TH), TH), :], cot, ld.at[2]
    )
    m1_load = pltpu.make_async_copy(m1_hbm, m1v, ld.at[3])
    m2_load = pltpu.make_async_copy(m2_hbm, m2v, ld.at[4])

    def w_load(b):
        return pltpu.make_async_copy(
            w_hbm.at[:, pl.ds(pl.multiple_of(b * CB, CB), CB)], wv.at[b], ld_w.at[b]
        )

    for copy in ctx_loads:
        copy.start()
    each_block(NB2, lambda b: w_load(b).start())
    cot_load.start()
    m1_load.start()
    m2_load.start()

    barrier = pltpu.get_barrier_semaphore()
    peers = [("dp_3", oc), ("mp", om), ("dp_1", oy)]
    peers += [("dp_2", away(x, d, NX)) for d in range(1, NX)]
    peers += [("dp_0", away(z, d, NZ)) for d in range(1, NZ)]
    for axis, peer in peers:
        pl.semaphore_signal(barrier, inc=1, device_id={axis: peer}, device_id_type=MESH)
    pl.semaphore_wait(barrier, len(peers))

    for copy in ctx_loads:
        copy.wait()

    def ctx_swap():
        return send(ctx_o, ctx_s, c_sem.at[0], c_sem.at[1], "dp_3", oc)

    ctx_swap().start()

    def partial_send(b):
        return send(psend.at[b], precv.at[b], p_s.at[b], p_r.at[b], "mp", om)

    def project_theirs(b):
        w_load(b).wait()
        psend[b] = dot_nn(ctx_o[om], wv[b]).astype(BF16)
        partial_send(b).start()

    each_block(NB2, project_theirs)

    cot_load.wait()
    ssr[...] = jnp.zeros_like(ssr)
    spr[...] = jnp.zeros_like(spr)
    gz[z] = jnp.zeros(gz.shape[1:], F32)

    def columns(b):
        return pl.ds(pl.multiple_of(b * CB, CB), CB)

    def project_ours(b):
        att[b] = dot_nn(ctx_o[m], wv[b])

    each_block(NB2, project_ours)

    def add_theirs(b):
        partial_send(b).wait_recv()
        a = att[b] + precv[b].astype(F32)
        att[b] = a
        s = cot[:, columns(b)].astype(F32) * gain_ref[:, columns(b)]
        sq, pr = a * a, a * s
        for k in range(CB // 128):
            ssr[...] += sq[:, k * 128 : (k + 1) * 128]
            spr[...] += pr[:, k * 128 : (k + 1) * 128]

    each_block(NB2, add_theirs)

    inverse = lax.rsqrt(jnp.sum(ssr[...], axis=1, keepdims=True) / D + norm_floor)
    mean_sn = inverse * (jnp.sum(spr[...], axis=1, keepdims=True) / D)

    def ga_send(h, j):
        return send(gaf.at[h, j, m], gaf.at[h, j, m], ga_s.at[h, j], ga_r.at[h, j], "mp", om)

    def ga_wait(h, j):
        return send(gaf.at[h, j, om], gaf.at[h, j, om], ga_s.at[h, j], ga_r.at[h, j], "mp", om)

    def side_send(j, k, who):
        return send(gaf.at[oc, j, who], gas.at[j, who], sa_s.at[j, k], sa_r.at[j, k], "dp_3", oc)

    def side_wait(j, k, who):
        return send(gas.at[j, who], gas.at[j, who], sa_s.at[j, k], sa_r.at[j, k], "dp_3", oc)

    def norm_gradient(j):
        for h in range(2):
            b = h * NB + j
            a = att[b]
            u = cot[:, columns(b)].astype(F32)
            s = u * gain_ref[:, columns(b)]
            normed = a * inverse
            gaf[h, j, m] = (inverse * (s - normed * mean_sn)).astype(BF16)
            ga_send(h, j).start()
            gz[z, pl.ds(b, 1), :] = jnp.sum(u * normed, axis=0, keepdims=True)
        side_send(j, 0, m).start()

    each_block(NB, norm_gradient)

    def gain_hop(buf, axis, me, n, ss, rs):
        return [
            send(buf.at[me], buf.at[me], ss.at[d], rs.at[d], axis, away(me, d, n)) for d in range(1, n)
        ]

    def gain_wait(buf, axis, me, n, ss, rs):
        for d in range(1, n):
            src = away(me, n - d, n)
            send(buf.at[src], buf.at[src], ss.at[d], rs.at[d], axis, src).wait_recv()

    hops = [
        (gz, "dp_0", z, NZ, gz_s, gz_r),
        (gx, "dp_2", x, NX, gx_s, gx_r),
        (gy, "dp_1", yl, NY, gt_s.at[0], gt_r.at[0]),
        (gm, "mp", m, 2, gt_s.at[1], gt_r.at[1]),
        (gk, "dp_3", c, 2, gt_s.at[2], gt_r.at[2]),
    ]

    def summed(buf, n):
        total = buf[0]
        for i in range(1, n):
            total = total + buf[i]
        return total

    for copy in gain_hop(*hops[0]):
        copy.start()

    def gain_stage(k):
        buf, _, _, n, _, _ = hops[k]
        gain_wait(*hops[k])
        total = summed(buf, n)
        if k + 1 < len(hops):
            nxt = hops[k + 1]
            nxt[0][nxt[2]] = total
            for copy in gain_hop(*nxt):
                copy.start()
        else:
            for b in range(NB2):
                gg_ref[:, b * CB : (b + 1) * CB] = total[b : b + 1, :]

    ctx_swap().wait_recv()

    def gather_grad_attn(j):
        ga_wait(0, j).wait_recv()
        ga_wait(1, j).wait_recv()
        side_send(j, 1, om).start()

    def x1_send(j, k):
        part = pl.ds(k * HZ, HZ)
        return send(
            grad.at[j, across, part], r1.at[j, k], x1_s.at[j, k], x1_r.at[j, k], "dp_2", right if k == 0 else left
        )

    def x2_send(j, k):
        peer = right if k == 0 else left
        return send(grad.at[j, peer], r2.at[j, k], x2_s.at[j, k], x2_r.at[j, k], "dp_2", peer)

    def z_send(j, d):
        peer = away(z, d, NZ)
        return send(zs.at[j, peer], zr.at[j, d], z_s.at[j, d], z_r.at[j, d], "dp_0", peer)

    def y_send(j):
        return send(yt.at[j, oy], yr.at[j], y_s.at[j], y_r.at[j], "dp_1", oy)

    def weight_grad(j):
        side_wait(j, 0, m).wait_recv()
        side_wait(j, 1, om).wait_recv()
        ours = gaf[c, j].reshape(T, CB)
        theirs = gas[j].reshape(T, CB)
        per = QR // (NX * 16)
        for q in range(H // QR):
            cols = slice(q * QR, (q + 1) * QR)
            part = dot_tn(ctx_o[:, :, cols].reshape(T, QR), ours)
            part = part + dot_tn(ctx_s[:, :, cols].reshape(T, QR), theirs)
            part = part.reshape(per, NX, 16, CB).astype(BF16)
            for k in range(NX):
                grad[j, k, q * per : (q + 1) * per] = part[:, k]
        x1_send(j, 0).start()
        x1_send(j, 1).start()

    def x_first(j):
        x1_send(j, 0).wait_recv()
        x1_send(j, 1).wait_recv()
        grad[j, right, :HZ] = (grad[j, right, :HZ].astype(F32) + r1[j, 0].astype(F32)).astype(BF16)
        grad[j, left, HZ:] = (grad[j, left, HZ:].astype(F32) + r1[j, 1].astype(F32)).astype(BF16)
        x2_send(j, 0).start()
        x2_send(j, 1).start()

    def x_second(j):
        x2_send(j, 0).wait_recv()
        x2_send(j, 1).wait_recv()
        total = grad[j, x].astype(F32) + r2[j, 0].astype(F32) + r2[j, 1].astype(F32)
        zs[j] = total.astype(BF16).reshape(NZ, NY, 16, CB)
        for d in range(1, NZ):
            z_send(j, d).start()

    def z_sum(j):
        for d in range(1, NZ):
            z_send(j, d).wait_recv()
        total = zs[j, z].astype(F32)
        for d in range(1, NZ):
            total = total + zr[j, d].astype(F32)
        yt[j] = total
        y_send(j).start()

    def context_grad(k):
        rows = pl.ds(pl.multiple_of(k * QR, QR), QR)
        total = None
        for h in range(2):
            for j in range(NB):
                term = dot_nt(gaf[h, j].reshape(T, CB), wv[h * NB + j, rows, :])
                total = term if total is None else total + term
        gc_ref[:, rows] = total.astype(BF16)

    stages = [z_sum, x_second, x_first, weight_grad, gather_grad_attn]

    def step(t):
        for depth, stage in enumerate(stages):
            lag = len(stages) - 1 - depth

            @pl.when((t >= lag) & (t < NB + lag))
            def _():
                stage(t - lag)

        for k in range(len(hops)):

            @pl.when(t == k + 1)
            def _():
                gain_stage(k)

        @pl.when((t >= NB) & (t < NB + H // QR))
        def _():
            context_grad(t - NB)

    each_block(NB + max(len(stages) - 1, len(hops), H // QR), step)

    def finish(j):
        y_send(j).wait_recv()
        total = yt[j, yl] + yr[j]
        fs[0, j] = total[:8]
        fs[1, j] = total[8:]

    each_block(NB, finish)

    def core_swap():
        return send(fs.at[oc], gr.at[c], f_sem.at[0], f_sem.at[1], "dp_3", oc)

    core_swap().start()
    gr[c] = fs[c]
    m1_load.wait()
    m2_load.wait()
    send(gr.at[oc], gr.at[oc], f_sem.at[0], f_sem.at[1], "dp_3", oc).wait_recv()
    row = pl.multiple_of(((z * NY + yl) * NX + x) * 16, 16)
    for b in range(NB2):
        cols = slice(b * CB, (b + 1) * CB)
        g = gr[b // NB, b % NB]
        first = beta_one * m1v[:, cols] + (1.0 - beta_one) * g
        second = beta_two * m2v[:, cols] + (1.0 - beta_two) * g * g
        both = wv[b, pl.ds(row, 16), :].astype(F32)
        master = jnp.where(c == 0, both[:8], both[8:])
        n1_ref[:, cols] = first
        n2_ref[:, cols] = second
        nw_ref[:, cols] = (master - learn_rate * first / (jnp.sqrt(second) + adam_floor)).astype(BF16)

    ctx_swap().wait_send()
    core_swap().wait_send()
    each_block(NB2, lambda b: partial_send(b).wait_send())
    for hop in hops:
        for copy in gain_hop(*hop):
            copy.wait_send()

    def drain(j):
        for h in range(2):
            ga_send(h, j).wait_send()
            x1_send(j, h).wait_send()
            x2_send(j, h).wait_send()
        side_send(j, 0, m).wait_send()
        side_send(j, 1, om).wait_send()
        for d in range(1, NZ):
            z_send(j, d).wait_send()
        y_send(j).wait_send()

    each_block(NB, drain)


def per_device(sizes, block, context, out_weight, cotangent, norm_gain, first_moment, second_moment):
    NZ, NY, NX = sizes
    T, H = context.shape
    D = out_weight.shape[1]
    TH, CB = T // 2, block
    NB = D // (2 * CB)
    NB2 = 2 * NB
    ZY = NZ * NY
    rows8 = (NB2 + 7) // 8 * 8
    dims = (NZ, NY, NX, TH, H, D, NB, CB)
    dma = pltpu.SemaphoreType.DMA
    scratch = [
        pltpu.VMEM((2, TH, H), BF16),
        pltpu.VMEM((2, TH, H), BF16),
        pltpu.VMEM((NB2, H, CB), BF16),
        pltpu.VMEM((TH, D), BF16),
        pltpu.VMEM((NB2, TH, CB), F32),
        pltpu.VMEM((NB2, TH, CB), BF16),
        pltpu.VMEM((NB2, TH, CB), BF16),
        pltpu.VMEM((TH, 128), F32),
        pltpu.VMEM((TH, 128), F32),
        pltpu.VMEM((2, NB, 2, TH, CB), BF16),
        pltpu.VMEM((NB, 2, TH, CB), BF16),
        pltpu.VMEM((NB, NX, ZY, 16, CB), BF16),
        pltpu.VMEM((NB, 2, ZY // 2, 16, CB), BF16),
        pltpu.VMEM((NB, 2, ZY, 16, CB), BF16),
        pltpu.VMEM((NB, NZ, NY, 16, CB), BF16),
        pltpu.VMEM((NB, NZ, NY, 16, CB), BF16),
        pltpu.VMEM((NB, NY, 16, CB), F32),
        pltpu.VMEM((NB, 16, CB), F32),
        pltpu.VMEM((2, NB, 8, CB), F32),
        pltpu.VMEM((2, NB, 8, CB), F32),
        pltpu.VMEM((8, D), F32),
        pltpu.VMEM((8, D), F32),
        pltpu.VMEM((NZ, rows8, CB), F32),
        pltpu.VMEM((NX, rows8, CB), F32),
        pltpu.VMEM((NY, rows8, CB), F32),
        pltpu.VMEM((2, rows8, CB), F32),
        pltpu.VMEM((2, rows8, CB), F32),
        dma((NB2,)), dma((5,)), dma((2,)),
        dma((NB2,)), dma((NB2,)),
        dma((2, NB)), dma((2, NB)),
        dma((NB, 2)), dma((NB, 2)),
        dma((NB, 2)), dma((NB, 2)),
        dma((NB, 2)), dma((NB, 2)),
        dma((NB, NZ)), dma((NB, NZ)),
        dma((NB,)), dma((NB,)),
        dma((2,)),
        dma((NZ,)), dma((NZ,)),
        dma((NX,)), dma((NX,)),
        dma((3, 2)), dma((3, 2)),
    ]
    any_space = pl.BlockSpec(memory_space=pl.ANY)
    vmem = pl.BlockSpec(memory_space=pltpu.VMEM)
    nw, n1, n2, gg, gc = pl.pallas_call(
        functools.partial(kernel, dims),
        out_shape=[
            jax.ShapeDtypeStruct((8, D), BF16),
            jax.ShapeDtypeStruct((8, D), F32),
            jax.ShapeDtypeStruct((8, D), F32),
            jax.ShapeDtypeStruct((1, D), F32),
            jax.ShapeDtypeStruct((T, H), BF16),
        ],
        in_specs=[any_space, any_space, any_space, vmem, any_space, any_space],
        out_specs=[vmem] * 5,
        scratch_shapes=scratch,
        compiler_params=pltpu.CompilerParams(
            collective_id=0, has_side_effects=True, vmem_limit_bytes=60 * 1024 * 1024
        ),
        name="step",
    )(context, out_weight, cotangent, norm_gain.reshape(1, D), first_moment[0], second_moment[0])
    return (nw[None], n1[None], n2[None], gg.reshape(D), gc)


def build(finer, block):
    sizes = tuple(finer.shape[a] for a in ("dp_0", "dp_1", "dp_2"))
    placed = (P(DP, "mp"), P("mp", None), P(DP, None), P(), P("mp", DP, None), P("mp", DP, None))
    return jax.shard_map(
        functools.partial(per_device, sizes, block),
        mesh=finer,
        in_specs=placed,
        out_specs=(P("mp", DP, None), P("mp", DP, None), P("mp", DP, None), P(), P(DP, "mp")),
        check_vma=False,
    )


def solution(mesh):
    finer = Mesh(
        mesh.devices.reshape(8, 2, 4, 2, mesh.shape["mp"]), ("dp_0", "dp_1", "dp_2", "dp_3", "mp")
    )
    return build(finer, 256)
```

time: 489 us -> 119 us (0.24)
  the two profiles are of different devices: /device:TPU:16 before, /device:TPU:1 now
where the time goes in v1:
time: 119 us; the launch traced here: 118 us
  Pallas kernels  108 us (91%)
  local copies, waits for them, and re-layouts  7.84 us (7%)
  other arithmetic  1.36 us (1%)
    pallas_call x1, Pallas kernels, per_device(): pl.pallas_call(functools.partial(kernel, dims), out_shape=[jax.ShapeDtype...  108 us
    unnamed x4, local copies, waits for them, and re-layouts  6.51 us

profile of v1, /device:TPU:1, one launch (start us, length us, event | category | flops | bytes accessed | tf_op | source)
XLA Modules:
  0.0 118.1 jit_solution(8206400985029972677)
XLA Ops:
  0.6 1.3 %reshape.16.gain_ref = f32[1,3584]{1,0:T(1,128)} reshape(f32[3584]{0:T(1024)} %param.9) | data formatting | bytes 28672 | tf_op jit(solution)/shard_map/reshape | solution.py:437
  2.0 108.2 %step.1 = (bf16[8,3584]{1,0:T(8,128)(2,1)}, f32[8,3584]{1,0:T(8,128)}, f32[8,3584]{1,0:T(8,128)}, f32[1,3584]{1,0:T(1,128)}, bf16[320,1024]{1,0:T(8,128)(2,1)}) custom-call(bf16[320,1024]{1,0:T(8,128)(2,1)} %ctx_hbm.1, bf16[1024,3584]{1,0:T(8,128)(2,1)} %w_hbm.1, bf16[320,3584]{1,0:T(8,128)(2,1)} %cot_hbm.1, f32[1,3584]{1,0:T(1,128)} %reshape.16.gain_ref, ...), custom_call_target="tpu_custom_call" | custom-call | tf_op jit(solution)/shard_map/step/pallas_call | solution.py:421
  110.2 1.4 %reduce = f32[3584]{0:T(1024)} reduce(f32[1,3584]{1,0:T(1,128)} %get-tuple-element.13, f32[]{:T(128)} %constant.4), dimensions={0}, to_apply=%get-tuple-element.13.reduce_sub_computation | reduce | bytes 28676 | tf_op jit(solution)/shard_map/step/pallas_call | solution.py:421
  111.6 1.4 %copy.15 = bf16[1,8,3584]{2,1,0:T(8,128)(2,1)} copy(bf16[1,8,3584]{2,1,0:T(8,128)(2,1)} %bitcast.9) | data formatting | bytes 114688
  113.0 1.6 %copy.16 = f32[1,8,3584]{2,1,0:T(8,128)} copy(f32[1,8,3584]{2,1,0:T(8,128)} %bitcast.8) | data formatting | bytes 229376
  114.5 1.6 %copy.17 = f32[1,8,3584]{2,1,0:T(8,128)} copy(f32[1,8,3584]{2,1,0:T(8,128)} %bitcast.7) | data formatting | bytes 229376
  116.1 2.0 %copy.18 = bf16[320,1024]{1,0:T(8,128)(2,1)} copy(bf16[320,1024]{1,0:T(8,128)(2,1)} %get-tuple-element.24) | data formatting | bytes 1310720

commit v2 on v1

--- a/solution.py
+++ b/solution.py
@@ -50,9 +50,9 @@
     ctx_hbm, w_hbm, cot_hbm, gain_ref, m1_hbm, m2_hbm,
     nw_ref, n1_ref, n2_ref, gg_ref, gc_ref,
     ctx_o, ctx_s, wv, cot, att, psend, precv, ssr, spr, gaf, gas,
-    grad, r1, r2, zs, zr, yt, yr, fs, gr, m1v, m2v, gz, gx, gy, gm, gk,
+    grad, r1, r2, zs, zr, fs, gr, m1v, m2v, gz, gx, gy, gm, gk,
     ld_w, ld, c_sem, p_s, p_r, ga_s, ga_r, sa_s, sa_r, x1_s, x1_r, x2_s, x2_r,
-    z_s, z_r, y_s, y_r, f_sem, gz_s, gz_r, gx_s, gx_r, gt_s, gt_r,
+    z_s, z_r, f_s, f_r, gz_s, gz_r, gx_s, gx_r, gt_s, gt_r,
 ):
     NZ, NY, NX, TH, H, D, NB, CB = dims
     NB2 = 2 * NB
@@ -69,7 +69,8 @@
         return lax.rem(me + d, n)
 
     right, left, across = away(x, 1, NX), away(x, NX - 1, NX), away(x, 2, NX)
-    om, oc, oy = 1 - m, 1 - c, 1 - yl
+    om, oc = 1 - m, 1 - c
+    owners = [(d, e) for d in range(NZ) for e in range(NY) if (d, e) != (0, 0)]
 
     def each_block(n, body):
         def step(i, carry):
@@ -100,15 +101,17 @@
     m2_load.start()
 
     barrier = pltpu.get_barrier_semaphore()
-    peers = [("dp_3", oc), ("mp", om), ("dp_1", oy)]
-    peers += [("dp_2", away(x, d, NX)) for d in range(1, NX)]
-    peers += [("dp_0", away(z, d, NZ)) for d in range(1, NZ)]
-    for axis, peer in peers:
-        pl.semaphore_signal(barrier, inc=1, device_id={axis: peer}, device_id_type=MESH)
-    pl.semaphore_wait(barrier, len(peers))
-
-    for copy in ctx_loads:
-        copy.wait()
+    peers = [{"dp_3": oc}, {"mp": om}]
+    peers += [{"dp_2": away(x, d, NX)} for d in range(1, NX)]
+    peers += [{"dp_0": away(z, d, NZ), "dp_1": away(yl, e, NY)} for d, e in owners]
+    for peer in peers:
+        pl.semaphore_signal(barrier, inc=1, device_id=peer, device_id_type=MESH)
+    with jax.named_scope("greet"):
+        pl.semaphore_wait(barrier, len(peers))
+
+    with jax.named_scope("ctx_wait"):
+        for copy in ctx_loads:
+            copy.wait()
 
     def ctx_swap():
         return send(ctx_o, ctx_s, c_sem.at[0], c_sem.at[1], "dp_3", oc)
@@ -123,7 +126,8 @@
         psend[b] = dot_nn(ctx_o[om], wv[b]).astype(BF16)
         partial_send(b).start()
 
-    each_block(NB2, project_theirs)
+    with jax.named_scope("project_theirs"):
+        each_block(NB2, project_theirs)
 
     cot_load.wait()
     ssr[...] = jnp.zeros_like(ssr)
@@ -136,10 +140,12 @@
     def project_ours(b):
         att[b] = dot_nn(ctx_o[m], wv[b])
 
-    each_block(NB2, project_ours)
+    with jax.named_scope("project_ours"):
+        each_block(NB2, project_ours)
 
     def add_theirs(b):
-        partial_send(b).wait_recv()
+        with jax.named_scope("wait_partial"):
+            partial_send(b).wait_recv()
         a = att[b] + precv[b].astype(F32)
         att[b] = a
         s = cot[:, columns(b)].astype(F32) * gain_ref[:, columns(b)]
@@ -148,7 +154,8 @@
             ssr[...] += sq[:, k * 128 : (k + 1) * 128]
             spr[...] += pr[:, k * 128 : (k + 1) * 128]
 
-    each_block(NB2, add_theirs)
+    with jax.named_scope("add_theirs"):
+        each_block(NB2, add_theirs)
 
     inverse = lax.rsqrt(jnp.sum(ssr[...], axis=1, keepdims=True) / D + norm_floor)
     mean_sn = inverse * (jnp.sum(spr[...], axis=1, keepdims=True) / D)
@@ -177,7 +184,8 @@
             gz[z, pl.ds(b, 1), :] = jnp.sum(u * normed, axis=0, keepdims=True)
         side_send(j, 0, m).start()
 
-    each_block(NB, norm_gradient)
+    with jax.named_scope("norm_gradient"):
+        each_block(NB, norm_gradient)
 
     def gain_hop(buf, axis, me, n, ss, rs):
         return [
@@ -236,12 +244,22 @@
         peer = right if k == 0 else left
         return send(grad.at[j, peer], r2.at[j, k], x2_s.at[j, k], x2_r.at[j, k], "dp_2", peer)
 
-    def z_send(j, d):
-        peer = away(z, d, NZ)
-        return send(zs.at[j, peer], zr.at[j, d], z_s.at[j, d], z_r.at[j, d], "dp_0", peer)
-
-    def y_send(j):
-        return send(yt.at[j, oy], yr.at[j], y_s.at[j], y_r.at[j], "dp_1", oy)
+    def z_send(j, d, e):
+        zp, yp = away(z, d, NZ), away(yl, e, NY)
+        return pltpu.make_async_remote_copy(
+            src_ref=zs.at[j, zp, yp],
+            dst_ref=zr.at[j, d, e],
+            send_sem=z_s.at[j, d, e],
+            recv_sem=z_r.at[j, d, e],
+            device_id={"dp_0": zp, "dp_1": yp},
+            device_id_type=MESH,
+        )
+
+    def core_send(j):
+        return send(fs.at[oc, j], gr.at[c, j], f_s.at[j], f_r.at[j], "dp_3", oc)
+
+    def core_wait(j):
+        return send(gr.at[oc, j], gr.at[oc, j], f_s.at[j], f_r.at[j], "dp_3", oc)
 
     def weight_grad(j):
         side_wait(j, 0, m).wait_recv()
@@ -272,17 +290,18 @@
         x2_send(j, 1).wait_recv()
         total = grad[j, x].astype(F32) + r2[j, 0].astype(F32) + r2[j, 1].astype(F32)
         zs[j] = total.astype(BF16).reshape(NZ, NY, 16, CB)
-        for d in range(1, NZ):
-            z_send(j, d).start()
+        for d, e in owners:
+            z_send(j, d, e).start()
 
     def z_sum(j):
-        for d in range(1, NZ):
-            z_send(j, d).wait_recv()
-        total = zs[j, z].astype(F32)
-        for d in range(1, NZ):
-            total = total + zr[j, d].astype(F32)
-        yt[j] = total
-        y_send(j).start()
+        for d, e in owners:
+            z_send(j, d, e).wait_recv()
+        total = zs[j, z, yl].astype(F32)
+        for d, e in owners:
+            total = total + zr[j, d, e].astype(F32)
+        fs[0, j] = total[:8]
+        fs[1, j] = total[8:]
+        core_send(j).start()
 
     def context_grad(k):
         rows = pl.ds(pl.multiple_of(k * QR, QR), QR)
@@ -293,44 +312,36 @@
                 total = term if total is None else total + term
         gc_ref[:, rows] = total.astype(BF16)
 
-    stages = [z_sum, x_second, x_first, weight_grad, gather_grad_attn]
+    stages = [(weight_grad, 1), (x_first, 2), (x_second, 4), (z_sum, 6), (gather_grad_attn, 0)]
+    gain_steps = (2, 4, NB + 1, NB + 2, NB + 3)
 
     def step(t):
-        for depth, stage in enumerate(stages):
-            lag = len(stages) - 1 - depth
+        for stage, lag in stages:
 
             @pl.when((t >= lag) & (t < NB + lag))
             def _():
-                stage(t - lag)
-
-        for k in range(len(hops)):
-
-            @pl.when(t == k + 1)
+                with jax.named_scope(stage.__name__):
+                    stage(t - lag)
+
+        for k, when in enumerate(gain_steps):
+
+            @pl.when(t == when)
             def _():
-                gain_stage(k)
+                with jax.named_scope("gain_stage"):
+                    gain_stage(k)
 
         @pl.when((t >= NB) & (t < NB + H // QR))
         def _():
-            context_grad(t - NB)
-
-    each_block(NB + max(len(stages) - 1, len(hops), H // QR), step)
-
-    def finish(j):
-        y_send(j).wait_recv()
-        total = yt[j, yl] + yr[j]
-        fs[0, j] = total[:8]
-        fs[1, j] = total[8:]
-
-    each_block(NB, finish)
-
-    def core_swap():
-        return send(fs.at[oc], gr.at[c], f_sem.at[0], f_sem.at[1], "dp_3", oc)
-
-    core_swap().start()
+            with jax.named_scope("context_grad"):
+                context_grad(t - NB)
+
+    each_block(NB + 6, step)
+
     gr[c] = fs[c]
     m1_load.wait()
     m2_load.wait()
-    send(gr.at[oc], gr.at[oc], f_sem.at[0], f_sem.at[1], "dp_3", oc).wait_recv()
+    with jax.named_scope("core_wait"):
+        each_block(NB, lambda j: core_wait(j).wait_recv())
     row = pl.multiple_of(((z * NY + yl) * NX + x) * 16, 16)
     for b in range(NB2):
         cols = slice(b * CB, (b + 1) * CB)
@@ -344,7 +355,6 @@
         nw_ref[:, cols] = (master - learn_rate * first / (jnp.sqrt(second) + adam_floor)).astype(BF16)
 
     ctx_swap().wait_send()
-    core_swap().wait_send()
     each_block(NB2, lambda b: partial_send(b).wait_send())
     for hop in hops:
         for copy in gain_hop(*hop):
@@ -357,11 +367,39 @@
             x2_send(j, h).wait_send()
         side_send(j, 0, m).wait_send()
         side_send(j, 1, om).wait_send()
-        for d in range(1, NZ):
-            z_send(j, d).wait_send()
-        y_send(j).wait_send()
-
-    each_block(NB, drain)
+        for d, e in owners:
+            z_send(j, d, e).wait_send()
+        core_send(j).wait_send()
+
+    with jax.named_scope("drain"):
+        each_block(NB, drain)
+
+
+def deliver(*refs):
+    n = (len(refs) - 1) // 3
+    src, dst, held, sem = refs[:n], refs[n : 2 * n], refs[2 * n : 3 * n], refs[-1]
+    into = [pltpu.make_async_copy(s, h, sem.at[i]) for i, (s, h) in enumerate(zip(src, held))]
+    out = [pltpu.make_async_copy(h, d, sem.at[n + i]) for i, (h, d) in enumerate(zip(held, dst))]
+    for copy in into:
+        copy.start()
+    for first, second in zip(into, out):
+        first.wait()
+        second.start()
+    for copy in out:
+        copy.wait()
+
+
+def delivered(arrays):
+    space = pl.BlockSpec(memory_space=pl.ANY)
+    return pl.pallas_call(
+        deliver,
+        out_shape=[jax.ShapeDtypeStruct(a.shape, a.dtype) for a in arrays],
+        in_specs=[space] * len(arrays),
+        out_specs=[space] * len(arrays),
+        scratch_shapes=[pltpu.VMEM(a.shape, a.dtype) for a in arrays]
+        + [pltpu.SemaphoreType.DMA((2 * len(arrays),))],
+        name="deliver",
+    )(*arrays)
 
 
 def per_device(sizes, block, context, out_weight, cotangent, norm_gain, first_moment, second_moment):
@@ -392,8 +430,6 @@
         pltpu.VMEM((NB, 2, ZY, 16, CB), BF16),
         pltpu.VMEM((NB, NZ, NY, 16, CB), BF16),
         pltpu.VMEM((NB, NZ, NY, 16, CB), BF16),
-        pltpu.VMEM((NB, NY, 16, CB), F32),
-        pltpu.VMEM((NB, 16, CB), F32),
         pltpu.VMEM((2, NB, 8, CB), F32),
         pltpu.VMEM((2, NB, 8, CB), F32),
         pltpu.VMEM((8, D), F32),
@@ -409,16 +445,15 @@
         dma((NB, 2)), dma((NB, 2)),
         dma((NB, 2)), dma((NB, 2)),
         dma((NB, 2)), dma((NB, 2)),
-        dma((NB, NZ)), dma((NB, NZ)),
+        dma((NB, NZ, NY)), dma((NB, NZ, NY)),
         dma((NB,)), dma((NB,)),
-        dma((2,)),
         dma((NZ,)), dma((NZ,)),
         dma((NX,)), dma((NX,)),
         dma((3, 2)), dma((3, 2)),
     ]
     any_space = pl.BlockSpec(memory_space=pl.ANY)
     vmem = pl.BlockSpec(memory_space=pltpu.VMEM)
-    nw, n1, n2, gg, gc = pl.pallas_call(
+    results = pl.pallas_call(
         functools.partial(kernel, dims),
         out_shape=[
             jax.ShapeDtypeStruct((8, D), BF16),
@@ -435,6 +470,7 @@
         ),
         name="step",
     )(context, out_weight, cotangent, norm_gain.reshape(1, D), first_moment[0], second_moment[0])
+    nw, n1, n2, gg, gc = delivered(results)
     return (nw[None], n1[None], n2[None], gg.reshape(D), gc)
 
 

time: 119 us -> 99.5 us (0.84)
  Pallas kernels: 108 us -> 95.8 us
  local copies, waits for them, and re-layouts: 7.84 us -> 1.33 us
    pallas_call x1, Pallas kernels: 108 us -> 93.6 us  [per_device(): pl.pallas_call(functools.partial(kernel, dims), out_shape=[jax.ShapeDtype...]
    unnamed x4 -> x0, local copies, waits for them, and re-layouts: 6.51 us -> none
    pallas_call x0 -> x1, Pallas kernels: none -> 2.18 us  [delivered(): pl.pallas_call(deliver, out_shape=[jax.ShapeDtypeStruct(a.shape, a.dtype)...]
where the time goes in v2:
time: 99.5 us; the launch traced here: 99.2 us
  Pallas kernels  95.8 us (96%)
  other arithmetic  1.36 us (1%)
  local copies, waits for them, and re-layouts  1.33 us (1%)
    pallas_call x1, Pallas kernels, per_device(): pl.pallas_call(functools.partial(kernel, dims), out_shape=[jax.ShapeDtype...  93.6 us
    pallas_call x1, Pallas kernels, delivered(): pl.pallas_call(deliver, out_shape=[jax.ShapeDtypeStruct(a.shape, a.dtype)...  2.18 us

profile of v2, /device:TPU:1, one launch (start us, length us, event | category | flops | bytes accessed | tf_op | source)
XLA Modules:
  0.0 99.2 jit_solution(10200196499071655894)
XLA Ops:
  0.6 1.3 %reshape.16.gain_ref = f32[1,3584]{1,0:T(1,128)} reshape(f32[3584]{0:T(1024)} %param.9) | data formatting | bytes 28672 | tf_op jit(solution)/shard_map/reshape | solution.py:472
  2.0 93.6 %step.1 = (bf16[8,3584]{1,0:T(8,128)(2,1)}, f32[8,3584]{1,0:T(8,128)}, f32[8,3584]{1,0:T(8,128)}, f32[1,3584]{1,0:T(1,128)}, bf16[320,1024]{1,0:T(8,128)(2,1)}) custom-call(bf16[320,1024]{1,0:T(8,128)(2,1)} %ctx_hbm.1, bf16[1024,3584]{1,0:T(8,128)(2,1)} %w_hbm.1, bf16[320,3584]{1,0:T(8,128)(2,1)} %cot_hbm.1, f32[1,3584]{1,0:T(1,128)} %reshape.16.gain_ref, ...), custom_call_target="tpu_custom_call" | custom-call | tf_op jit(solution)/shard_map/step/pallas_call | solution.py:456
  95.6 2.2 %deliver.1 = (bf16[8,3584]{1,0:T(8,128)(2,1)}, f32[8,3584]{1,0:T(8,128)}, f32[8,3584]{1,0:T(8,128)}, f32[1,3584]{1,0:T(1,128)}, bf16[320,1024]{1,0:T(8,128)(2,1)}) custom-call(bf16[8,3584]{1,0:T(8,128)(2,1)} %get-tuple-element.15.refs_0_, f32[8,3584]{1,0:T(8,128)} %get-tuple-element.16.refs_1_, f32[8,3584]{1,0:T(8,128)} %get-tuple-element.17.refs_2_, ...), custom_call_target="tpu_custom_call" | custom-call | tf_op jit(solution)/shard_map/deliver/pallas_call | solution.py:394
  97.8 1.4 %reduce = f32[3584]{0:T(1024)} reduce(f32[1,3584]{1,0:T(1,128)} %get-tuple-element.23, f32[]{:T(128)} %constant.4), dimensions={0}, to_apply=%get-tuple-element.23.reduce_sub_computation | reduce | bytes 28676 | tf_op jit(solution)/shard_map/deliver/pallas_call | solution.py:394

commit v3 on v2

--- a/solution.py
+++ b/solution.py
@@ -20,6 +20,13 @@
 adam_floor = 1e-08
 
 QR = 256
+
+
+Z_LAGS = (1, 2, 4, 6, 8, 10)
+
+
+def z_blocks(n):
+    return (0, 2) if n > 2 else (0,)
 
 
 def dot_nn(a, b):
@@ -45,19 +52,25 @@
     )
 
 
+def landed(ref, sem):
+    pltpu.make_async_copy(ref, ref, sem).wait()
+
+
 def kernel(
     dims,
     ctx_hbm, w_hbm, cot_hbm, gain_ref, m1_hbm, m2_hbm,
-    nw_ref, n1_ref, n2_ref, gg_ref, gc_ref,
+    nw_hbm, n1_hbm, n2_hbm, gg_hbm, gc_hbm,
+    nw_ref, n1_ref, n2_ref, gg_ref, gcv,
     ctx_o, ctx_s, wv, cot, att, psend, precv, ssr, spr, gaf, gas,
-    grad, r1, r2, zs, zr, fs, gr, m1v, m2v, gz, gx, gy, gm, gk,
-    ld_w, ld, c_sem, p_s, p_r, ga_s, ga_r, sa_s, sa_r, x1_s, x1_r, x2_s, x2_r,
-    z_s, z_r, f_s, f_r, gz_s, gz_r, gx_s, gx_r, gt_s, gt_r,
+    grad, rx, rz, zs, zr, xs, xr, fs, gr, m1v, m2v, gz, gx, gy, gm, gk,
+    ld_w, ld, c_sem, p_s, p_r, ga_s, ga_r, sa_s, sa_r, x_s, x_r, zz_s, zz_r,
+    z_s, z_r, xo_s, xo_r, o_sem, f_s, f_r, gt_s, gt_r,
 ):
     NZ, NY, NX, TH, H, D, NB, CB = dims
+    ZB = z_blocks(NB)
+    NG = NZ * NY * NX
     NB2 = 2 * NB
     ZY = NZ * NY
-    HZ = ZY // 2
     T = 2 * TH
     z = lax.axis_index("dp_0")
     yl = lax.axis_index("dp_1")
@@ -68,9 +81,9 @@
     def away(me, d, n):
         return lax.rem(me + d, n)
 
-    right, left, across = away(x, 1, NX), away(x, NX - 1, NX), away(x, 2, NX)
     om, oc = 1 - m, 1 - c
     owners = [(d, e) for d in range(NZ) for e in range(NY) if (d, e) != (0, 0)]
+    x_owners = [(d, e) for d in range(NX) for e in range(NY) if (d, e) != (0, 0)]
 
     def each_block(n, body):
         def step(i, carry):
@@ -102,7 +115,7 @@
 
     barrier = pltpu.get_barrier_semaphore()
     peers = [{"dp_3": oc}, {"mp": om}]
-    peers += [{"dp_2": away(x, d, NX)} for d in range(1, NX)]
+    peers += [{"dp_2": away(x, d, NX), "dp_1": away(yl, e, NY)} for d, e in x_owners if d]
     peers += [{"dp_0": away(z, d, NZ), "dp_1": away(yl, e, NY)} for d, e in owners]
     for peer in peers:
         pl.semaphore_signal(barrier, inc=1, device_id=peer, device_id_type=MESH)
@@ -119,7 +132,7 @@
     ctx_swap().start()
 
     def partial_send(b):
-        return send(psend.at[b], precv.at[b], p_s.at[b], p_r.at[b], "mp", om)
+        return send(psend.at[b], precv.at[b], p_s.at[0], p_r.at[b], "mp", om)
 
     def project_theirs(b):
         w_load(b).wait()
@@ -161,16 +174,10 @@
     mean_sn = inverse * (jnp.sum(spr[...], axis=1, keepdims=True) / D)
 
     def ga_send(h, j):
-        return send(gaf.at[h, j, m], gaf.at[h, j, m], ga_s.at[h, j], ga_r.at[h, j], "mp", om)
-
-    def ga_wait(h, j):
-        return send(gaf.at[h, j, om], gaf.at[h, j, om], ga_s.at[h, j], ga_r.at[h, j], "mp", om)
-
-    def side_send(j, k, who):
-        return send(gaf.at[oc, j, who], gas.at[j, who], sa_s.at[j, k], sa_r.at[j, k], "dp_3", oc)
-
-    def side_wait(j, k, who):
-        return send(gas.at[j, who], gas.at[j, who], sa_s.at[j, k], sa_r.at[j, k], "dp_3", oc)
+        return send(gaf.at[h, j, m], gaf.at[h, j, m], ga_s.at[0], ga_r.at[j], "mp", om)
+
+    def side_send(j, who):
+        return send(gaf.at[oc, j, who], gas.at[j, who], sa_s.at[0], sa_r.at[j], "dp_3", oc)
 
     def norm_gradient(j):
         for h in range(2):
@@ -182,27 +189,26 @@
             gaf[h, j, m] = (inverse * (s - normed * mean_sn)).astype(BF16)
             ga_send(h, j).start()
             gz[z, pl.ds(b, 1), :] = jnp.sum(u * normed, axis=0, keepdims=True)
-        side_send(j, 0, m).start()
+        side_send(j, m).start()
 
     with jax.named_scope("norm_gradient"):
         each_block(NB, norm_gradient)
 
     def gain_hop(buf, axis, me, n, ss, rs):
         return [
-            send(buf.at[me], buf.at[me], ss.at[d], rs.at[d], axis, away(me, d, n)) for d in range(1, n)
+            send(buf.at[me], buf.at[me], ss, rs, axis, away(me, d, n)) for d in range(1, n)
         ]
 
     def gain_wait(buf, axis, me, n, ss, rs):
-        for d in range(1, n):
-            src = away(me, n - d, n)
-            send(buf.at[src], buf.at[src], ss.at[d], rs.at[d], axis, src).wait_recv()
+        if n > 1:
+            landed(buf.at[pl.ds(0, n - 1)], rs)
 
     hops = [
-        (gz, "dp_0", z, NZ, gz_s, gz_r),
-        (gx, "dp_2", x, NX, gx_s, gx_r),
-        (gy, "dp_1", yl, NY, gt_s.at[0], gt_r.at[0]),
-        (gm, "mp", m, 2, gt_s.at[1], gt_r.at[1]),
-        (gk, "dp_3", c, 2, gt_s.at[2], gt_r.at[2]),
+        (gz, "dp_0", z, NZ, gt_s.at[0], gt_r.at[0]),
+        (gx, "dp_2", x, NX, gt_s.at[1], gt_r.at[1]),
+        (gy, "dp_1", yl, NY, gt_s.at[2], gt_r.at[2]),
+        (gm, "mp", m, 2, gt_s.at[3], gt_r.at[3]),
+        (gk, "dp_3", c, 2, gt_s.at[4], gt_r.at[4]),
     ]
 
     def summed(buf, n):
@@ -230,78 +236,150 @@
     ctx_swap().wait_recv()
 
     def gather_grad_attn(j):
-        ga_wait(0, j).wait_recv()
-        ga_wait(1, j).wait_recv()
-        side_send(j, 1, om).start()
-
-    def x1_send(j, k):
-        part = pl.ds(k * HZ, HZ)
-        return send(
-            grad.at[j, across, part], r1.at[j, k], x1_s.at[j, k], x1_r.at[j, k], "dp_2", right if k == 0 else left
-        )
-
-    def x2_send(j, k):
-        peer = right if k == 0 else left
-        return send(grad.at[j, peer], r2.at[j, k], x2_s.at[j, k], x2_r.at[j, k], "dp_2", peer)
+        landed(gaf.at[:, j, om], ga_r.at[j])
+        side_send(j, om).start()
+
+    def ring(j, buf, slot, n, me, axis, ss, rs):
+        size, steps = NG // n, n // 2
+        half = size // 2
+
+        def rows(t, k):
+            far = steps + 1 - t
+            target = away(me, far if k == 0 else n - far, n)
+            if t == 1:
+                return pl.ds(target * size + k * half, half)
+            return pl.ds(target * size, size)
+
+        def hop(t, k):
+            peer = away(me, 1 if k == 0 else n - 1, n)
+            dst = buf.at[slot, t - 1, k, pl.ds(0, half)] if t == 1 else buf.at[slot, t - 1, k]
+            return send(
+                grad.at[j, rows(t, k)], dst, ss.at[slot], rs.at[slot, t - 1], axis, peer
+            )
+
+        def arrived(t, k):
+            return (buf[slot, t - 1, k, :half] if t == 1 else buf[slot, t - 1, k]).astype(F32)
+
+        def wait(t):
+            landed(buf.at[slot, 0, :, pl.ds(0, half)] if t == 1 else buf.at[slot, t - 1], rs.at[slot, t - 1])
+
+        def start(t):
+            for k in range(2):
+                hop(t, k).start()
+
+        def add_and_start(t):
+            wait(t - 1)
+            for k in range(2):
+                far = steps + 1 - t
+                target = away(me, far if k == 0 else n - far, n)
+                if t == 2:
+                    part = pl.ds(target * size + k * half, half)
+                else:
+                    part = pl.ds(target * size, size)
+                grad[j, part] = (grad[j, part].astype(F32) + arrived(t - 1, k)).astype(BF16)
+            start(t)
+
+        def total():
+            wait(steps)
+            return grad[j, pl.ds(me * size, size)].astype(F32) + arrived(steps, 0) + arrived(steps, 1)
+
+        def sent():
+            landed(grad.at[j, pl.ds(0, (2 * steps - 1) * size)], ss.at[slot])
+
+        return start, add_and_start, total, sent
+
+    def x_ring(j):
+        return ring(j, rx, j, NX, x, "dp_2", x_s, x_r)
+
+    def z_ring(i):
+        return ring(ZB[i], rz, i, NZ, z, "dp_0", zz_s, zz_r)
 
     def z_send(j, d, e):
         zp, yp = away(z, d, NZ), away(yl, e, NY)
         return pltpu.make_async_remote_copy(
             src_ref=zs.at[j, zp, yp],
-            dst_ref=zr.at[j, d, e],
-            send_sem=z_s.at[j, d, e],
-            recv_sem=z_r.at[j, d, e],
+            dst_ref=zr.at[j, d * NY + e],
+            send_sem=z_s.at[j],
+            recv_sem=z_r.at[j],
             device_id={"dp_0": zp, "dp_1": yp},
             device_id_type=MESH,
         )
 
     def core_send(j):
-        return send(fs.at[oc, j], gr.at[c, j], f_s.at[j], f_r.at[j], "dp_3", oc)
-
-    def core_wait(j):
-        return send(gr.at[oc, j], gr.at[oc, j], f_s.at[j], f_r.at[j], "dp_3", oc)
-
-    def weight_grad(j):
-        side_wait(j, 0, m).wait_recv()
-        side_wait(j, 1, om).wait_recv()
+        return send(fs.at[oc, j], gr.at[c, j], f_s.at[0], f_r.at[0], "dp_3", oc)
+
+    def weight_grad(j, z_first):
+        landed(gas.at[j], sa_r.at[j])
         ours = gaf[c, j].reshape(T, CB)
         theirs = gas[j].reshape(T, CB)
-        per = QR // (NX * 16)
+        per = QR // 16
         for q in range(H // QR):
             cols = slice(q * QR, (q + 1) * QR)
             part = dot_tn(ctx_o[:, :, cols].reshape(T, QR), ours)
             part = part + dot_tn(ctx_s[:, :, cols].reshape(T, QR), theirs)
-            part = part.reshape(per, NX, 16, CB).astype(BF16)
-            for k in range(NX):
-                grad[j, k, q * per : (q + 1) * per] = part[:, k]
-        x1_send(j, 0).start()
-        x1_send(j, 1).start()
+            part = part.astype(BF16)
+            if z_first:
+                grad[j, q * per : (q + 1) * per] = part.reshape(per, 16, CB)
+            else:
+                part = part.reshape(per // NX, NX, 16, CB)
+                for k in range(NX):
+                    at = k * ZY + q * (per // NX)
+                    grad[j, at : at + per // NX] = part[:, k]
+
+    def x_start(j):
+        weight_grad(j, False)
+        x_ring(j)[0](1)
 
     def x_first(j):
-        x1_send(j, 0).wait_recv()
-        x1_send(j, 1).wait_recv()
-        grad[j, right, :HZ] = (grad[j, right, :HZ].astype(F32) + r1[j, 0].astype(F32)).astype(BF16)
-        grad[j, left, HZ:] = (grad[j, left, HZ:].astype(F32) + r1[j, 1].astype(F32)).astype(BF16)
-        x2_send(j, 0).start()
-        x2_send(j, 1).start()
+        x_ring(j)[1](2)
 
     def x_second(j):
-        x2_send(j, 0).wait_recv()
-        x2_send(j, 1).wait_recv()
-        total = grad[j, x].astype(F32) + r2[j, 0].astype(F32) + r2[j, 1].astype(F32)
-        zs[j] = total.astype(BF16).reshape(NZ, NY, 16, CB)
+        zs[j] = x_ring(j)[2]().astype(BF16).reshape(NZ, NY, 16, CB)
         for d, e in owners:
             z_send(j, d, e).start()
 
-    def z_sum(j):
-        for d, e in owners:
-            z_send(j, d, e).wait_recv()
-        total = zs[j, z, yl].astype(F32)
-        for d, e in owners:
-            total = total + zr[j, d, e].astype(F32)
+    def z_start(i):
+        weight_grad(ZB[i], True)
+        z_ring(i)[0](1)
+
+    def z_last(i):
+        xs[i] = z_ring(i)[2]().astype(BF16).reshape(NY, NX, 16, CB)
+        for d, e in x_owners:
+            xo_send(i, d, e).start()
+
+    def x_sum(i):
+        landed(xr.at[i, pl.ds(1, NX * NY - 1)], xo_r.at[i])
+        total = xs[i, yl, x].astype(F32)
+        for d, e in x_owners:
+            total = total + xr[i, d * NY + e].astype(F32)
+        to_core(ZB[i], total)
+
+    def to_core(j, total):
         fs[0, j] = total[:8]
         fs[1, j] = total[8:]
         core_send(j).start()
+
+    def xo_send(i, d, e):
+        xp, yp = away(x, d, NX), away(yl, e, NY)
+        return pltpu.make_async_remote_copy(
+            src_ref=xs.at[i, yp, xp],
+            dst_ref=xr.at[i, d * NY + e],
+            send_sem=xo_s.at[i],
+            recv_sem=xo_r.at[i],
+            device_id={"dp_2": xp, "dp_1": yp},
+            device_id_type=MESH,
+        )
+
+    def z_sum(j):
+        landed(zr.at[j, pl.ds(1, ZY - 1)], z_r.at[j])
+        total = zs[j, z, yl].astype(F32)
+        for d, e in owners:
+            total = total + zr[j, d * NY + e].astype(F32)
+        to_core(j, total)
+
+    def context_out(k):
+        rows = pl.ds(pl.multiple_of(k * QR, QR), QR)
+        return pltpu.make_async_copy(gcv.at[k], gc_hbm.at[:, rows], o_sem.at[4])
 
     def context_grad(k):
         rows = pl.ds(pl.multiple_of(k * QR, QR), QR)
@@ -310,18 +388,41 @@
             for j in range(NB):
                 term = dot_nt(gaf[h, j].reshape(T, CB), wv[h * NB + j, rows, :])
                 total = term if total is None else total + term
-        gc_ref[:, rows] = total.astype(BF16)
-
-    stages = [(weight_grad, 1), (x_first, 2), (x_second, 4), (z_sum, 6), (gather_grad_attn, 0)]
+        gcv[k] = total.astype(BF16)
+        context_out(k).start()
+
+    steps_z = NZ // 2
+    stages = [(x_start, 1), (x_first, 2), (x_second, 4), (z_sum, 6)]
+    z_stages = [(z_start, Z_LAGS[0])]
+    for n in range(2, steps_z + 1):
+        z_stages.append((lambda i, n=n: z_ring(i)[1](n), Z_LAGS[n - 1]))
+    z_stages += [(z_last, Z_LAGS[steps_z]), (x_sum, Z_LAGS[steps_z + 1])]
     gain_steps = (2, 4, NB + 1, NB + 2, NB + 3)
+    last = max(NB + 6, max(ZB) + Z_LAGS[steps_z + 1] + 1)
 
     def step(t):
         for stage, lag in stages:
-
-            @pl.when((t >= lag) & (t < NB + lag))
+            mine = (t >= lag) & (t < NB + lag)
+            for b in ZB:
+                mine = mine & (t != b + lag)
+
+            @pl.when(mine)
             def _():
                 with jax.named_scope(stage.__name__):
                     stage(t - lag)
+
+        for stage, lag in z_stages:
+            for i, b in enumerate(ZB):
+
+                @pl.when(t == b + lag)
+                def _():
+                    with jax.named_scope(f"z{lag}"):
+                        stage(i)
+
+        @pl.when(t < NB)
+        def _():
+            with jax.named_scope("gather"):
+                gather_grad_attn(t)
 
         for k, when in enumerate(gain_steps):
 
@@ -335,13 +436,13 @@
             with jax.named_scope("context_grad"):
                 context_grad(t - NB)
 
-    each_block(NB + 6, step)
+    each_block(last, step)
 
     gr[c] = fs[c]
     m1_load.wait()
     m2_load.wait()
     with jax.named_scope("core_wait"):
-        each_block(NB, lambda j: core_wait(j).wait_recv())
+        landed(gr.at[oc], f_r.at[0])
     row = pl.multiple_of(((z * NY + yl) * NX + x) * 16, 16)
     for b in range(NB2):
         cols = slice(b * CB, (b + 1) * CB)
@@ -354,25 +455,36 @@
         n2_ref[:, cols] = second
         nw_ref[:, cols] = (master - learn_rate * first / (jnp.sqrt(second) + adam_floor)).astype(BF16)
 
+    outs = [
+        pltpu.make_async_copy(a, b, o_sem.at[i])
+        for i, (a, b) in enumerate([(nw_ref, nw_hbm), (n1_ref, n1_hbm), (n2_ref, n2_hbm), (gg_ref, gg_hbm)])
+    ]
+    for copy in outs:
+        copy.start()
+
     ctx_swap().wait_send()
-    each_block(NB2, lambda b: partial_send(b).wait_send())
+    landed(psend, p_s.at[0])
     for hop in hops:
-        for copy in gain_hop(*hop):
-            copy.wait_send()
+        if hop[3] > 1:
+            landed(hop[0].at[pl.ds(0, hop[3] - 1)], hop[4])
+
+    landed(gaf.at[:, :, m], ga_s.at[0])
+    landed(gas, sa_s.at[0])
+    landed(fs.at[oc], f_s.at[0])
 
     def drain(j):
-        for h in range(2):
-            ga_send(h, j).wait_send()
-            x1_send(j, h).wait_send()
-            x2_send(j, h).wait_send()
-        side_send(j, 0, m).wait_send()
-        side_send(j, 1, om).wait_send()
-        for d, e in owners:
-            z_send(j, d, e).wait_send()
-        core_send(j).wait_send()
-
-    with jax.named_scope("drain"):
-        each_block(NB, drain)
+        x_ring(j)[3]()
+        landed(zr.at[j, pl.ds(1, ZY - 1)], z_s.at[j])
+
+    for j in range(NB):
+        if j not in ZB:
+            drain(j)
+    for i in range(len(ZB)):
+        z_ring(i)[3]()
+        landed(xr.at[i, pl.ds(1, NX * NY - 1)], xo_s.at[i])
+    landed(gcv, o_sem.at[4])
+    for copy in outs:
+        copy.wait()
 
 
 def deliver(*refs):
@@ -410,10 +522,16 @@
     NB = D // (2 * CB)
     NB2 = 2 * NB
     ZY = NZ * NY
+    NZB = len(z_blocks(NB))
     rows8 = (NB2 + 7) // 8 * 8
     dims = (NZ, NY, NX, TH, H, D, NB, CB)
     dma = pltpu.SemaphoreType.DMA
     scratch = [
+        pltpu.VMEM((8, D), BF16),
+        pltpu.VMEM((8, D), F32),
+        pltpu.VMEM((8, D), F32),
+        pltpu.VMEM((1, D), F32),
+        pltpu.VMEM((H // QR, T, QR), BF16),
         pltpu.VMEM((2, TH, H), BF16),
         pltpu.VMEM((2, TH, H), BF16),
         pltpu.VMEM((NB2, H, CB), BF16),
@@ -425,11 +543,13 @@
         pltpu.VMEM((TH, 128), F32),
         pltpu.VMEM((2, NB, 2, TH, CB), BF16),
         pltpu.VMEM((NB, 2, TH, CB), BF16),
-        pltpu.VMEM((NB, NX, ZY, 16, CB), BF16),
-        pltpu.VMEM((NB, 2, ZY // 2, 16, CB), BF16),
-        pltpu.VMEM((NB, 2, ZY, 16, CB), BF16),
+        pltpu.VMEM((NB, NZ * NY * NX, 16, CB), BF16),
+        pltpu.VMEM((NB, NX // 2, 2, ZY, 16, CB), BF16),
+        pltpu.VMEM((NZB, NZ // 2, 2, NY * NX, 16, CB), BF16),
         pltpu.VMEM((NB, NZ, NY, 16, CB), BF16),
-        pltpu.VMEM((NB, NZ, NY, 16, CB), BF16),
+        pltpu.VMEM((NB, ZY, 16, CB), BF16),
+        pltpu.VMEM((NZB, NY, NX, 16, CB), BF16),
+        pltpu.VMEM((NZB, NX * NY, 16, CB), BF16),
         pltpu.VMEM((2, NB, 8, CB), F32),
         pltpu.VMEM((2, NB, 8, CB), F32),
         pltpu.VMEM((8, D), F32),
@@ -440,16 +560,16 @@
         pltpu.VMEM((2, rows8, CB), F32),
         pltpu.VMEM((2, rows8, CB), F32),
         dma((NB2,)), dma((5,)), dma((2,)),
-        dma((NB2,)), dma((NB2,)),
-        dma((2, NB)), dma((2, NB)),
-        dma((NB, 2)), dma((NB, 2)),
-        dma((NB, 2)), dma((NB, 2)),
-        dma((NB, 2)), dma((NB, 2)),
-        dma((NB, NZ, NY)), dma((NB, NZ, NY)),
+        dma((1,)), dma((NB2,)),
+        dma((1,)), dma((NB,)),
+        dma((1,)), dma((NB,)),
+        dma((NB,)), dma((NB, NX // 2)),
+        dma((NZB,)), dma((NZB, NZ // 2)),
         dma((NB,)), dma((NB,)),
-        dma((NZ,)), dma((NZ,)),
-        dma((NX,)), dma((NX,)),
-        dma((3, 2)), dma((3, 2)),
+        dma((NZB,)), dma((NZB,)),
+        dma((5,)),
+        dma((1,)), dma((1,)),
+        dma((5,)), dma((5,)),
     ]
     any_space = pl.BlockSpec(memory_space=pl.ANY)
     vmem = pl.BlockSpec(memory_space=pltpu.VMEM)
@@ -463,7 +583,7 @@
             jax.ShapeDtypeStruct((T, H), BF16),
         ],
         in_specs=[any_space, any_space, any_space, vmem, any_space, any_space],
-        out_specs=[vmem] * 5,
+        out_specs=[any_space] * 5,
         scratch_shapes=scratch,
         compiler_params=pltpu.CompilerParams(
             collective_id=0, has_side_effects=True, vmem_limit_bytes=60 * 1024 * 1024

time: 99.5 us -> 93.7 us (0.942)
  Pallas kernels: 95.8 us -> 90 us
    pallas_call x1, Pallas kernels: 93.6 us -> 87.8 us  [per_device(): pl.pallas_call(functools.partial(kernel, dims), out_shape=[jax.ShapeDtype...]
where the time goes in v3:
time: 93.7 us; the launch traced here: 93.3 us
  Pallas kernels  90 us (96%)
  other arithmetic  1.36 us (1%)
  local copies, waits for them, and re-layouts  1.33 us (1%)
    pallas_call x1, Pallas kernels, per_device(): pl.pallas_call(functools.partial(kernel, dims), out_shape=[jax.ShapeDtype...  87.8 us
    pallas_call x1, Pallas kernels, delivered(): pl.pallas_call(deliver, out_shape=[jax.ShapeDtypeStruct(a.shape, a.dtype)...  2.18 us

profile of v3, /device:TPU:1, one launch (start us, length us, event | category | flops | bytes accessed | tf_op | source)
XLA Modules:
  0.0 93.3 jit_solution(4850340776794094908)
XLA Ops:
  0.6 1.3 %reshape.16.gain_ref = f32[1,3584]{1,0:T(1,128)} reshape(f32[3584]{0:T(1024)} %param.9) | data formatting | bytes 28672 | tf_op jit(solution)/shard_map/reshape | solution.py:592
  2.0 87.8 %step.1 = (bf16[8,3584]{1,0:T(8,128)(2,1)}, f32[8,3584]{1,0:T(8,128)}, f32[8,3584]{1,0:T(8,128)}, f32[1,3584]{1,0:T(1,128)}, bf16[320,1024]{1,0:T(8,128)(2,1)}) custom-call(bf16[320,1024]{1,0:T(8,128)(2,1)} %ctx_hbm.1, bf16[1024,3584]{1,0:T(8,128)(2,1)} %w_hbm.1, bf16[320,3584]{1,0:T(8,128)(2,1)} %cot_hbm.1, f32[1,3584]{1,0:T(1,128)} %reshape.16.gain_ref, ...), custom_call_target="tpu_custom_call" | custom-call | tf_op jit(solution)/shard_map/step/pallas_call | solution.py:576
  89.8 2.2 %deliver.1 = (bf16[8,3584]{1,0:T(8,128)(2,1)}, f32[8,3584]{1,0:T(8,128)}, f32[8,3584]{1,0:T(8,128)}, f32[1,3584]{1,0:T(1,128)}, bf16[320,1024]{1,0:T(8,128)(2,1)}) custom-call(bf16[8,3584]{1,0:T(8,128)(2,1)} %get-tuple-element.15.refs_0_, f32[8,3584]{1,0:T(8,128)} %get-tuple-element.16.refs_1_, f32[8,3584]{1,0:T(8,128)} %get-tuple-element.17.refs_2_, ...), custom_call_target="tpu_custom_call" | custom-call | tf_op jit(solution)/shard_map/deliver/pallas_call | solution.py:506
  92.0 1.4 %reduce = f32[3584]{0:T(1024)} reduce(f32[1,3584]{1,0:T(1,128)} %get-tuple-element.23, f32[]{:T(128)} %constant.4), dimensions={0}, to_apply=%get-tuple-element.23.reduce_sub_computation | reduce | bytes 28676 | tf_op jit(solution)/shard_map/deliver/pallas_call | solution.py:506

commit v4 on v3

--- a/solution.py
+++ b/solution.py
@@ -22,11 +22,18 @@
 QR = 256
 
 
-Z_LAGS = (1, 2, 4, 6, 8, 10)
+Z_PLAN = {0: (1, 2, 4, 6, 8, 10), 1: (1, 2, 4, 6, 8, 9), 3: (1, 2, 4, 5, 7, 9)}
+
+
+AHEAD = 2
 
 
 def z_blocks(n):
-    return (0, 2) if n > 2 else (0,)
+    return [b for b in Z_PLAN if b < n - 1]
+
+
+def far_first(n):
+    return sorted(range(n), key=lambda d: -min(d, n - d))
 
 
 def dot_nn(a, b):
@@ -62,13 +69,14 @@
     nw_hbm, n1_hbm, n2_hbm, gg_hbm, gc_hbm,
     nw_ref, n1_ref, n2_ref, gg_ref, gcv,
     ctx_o, ctx_s, wv, cot, att, psend, precv, ssr, spr, gaf, gas,
-    grad, rx, rz, zs, zr, xs, xr, fs, gr, m1v, m2v, gz, gx, gy, gm, gk,
+    grad, own, ox, oz, rx, rz, zs, zr, xs, xr, fs, gr, m1v, m2v, gz, gx, gy, gm, gk,
     ld_w, ld, c_sem, p_s, p_r, ga_s, ga_r, sa_s, sa_r, x_s, x_r, zz_s, zz_r,
     z_s, z_r, xo_s, xo_r, o_sem, f_s, f_r, gt_s, gt_r,
 ):
     NZ, NY, NX, TH, H, D, NB, CB = dims
     ZB = z_blocks(NB)
     NG = NZ * NY * NX
+    TA = TH * 4 // 5 // 16 * 16
     NB2 = 2 * NB
     ZY = NZ * NY
     T = 2 * TH
@@ -82,8 +90,8 @@
         return lax.rem(me + d, n)
 
     om, oc = 1 - m, 1 - c
-    owners = [(d, e) for d in range(NZ) for e in range(NY) if (d, e) != (0, 0)]
-    x_owners = [(d, e) for d in range(NX) for e in range(NY) if (d, e) != (0, 0)]
+    owners = [(d, e) for d in far_first(NZ) for e in far_first(NY) if (d, e) != (0, 0)]
+    x_owners = [(d, e) for d in far_first(NX) for e in far_first(NY) if (d, e) != (0, 0)]
 
     def each_block(n, body):
         def step(i, carry):
@@ -131,8 +139,13 @@
 
     ctx_swap().start()
 
+    head, tail = slice(0, TA), slice(TA, TH)
+
     def partial_send(b):
-        return send(psend.at[b], precv.at[b], p_s.at[0], p_r.at[b], "mp", om)
+        return send(psend.at[b, head], precv.at[b, head], p_s.at[0], p_r.at[b], "mp", om)
+
+    def partial_rest():
+        return send(psend.at[:, tail], precv.at[:, tail], p_s.at[0], p_r.at[NB2], "mp", om)
 
     def project_theirs(b):
         w_load(b).wait()
@@ -142,6 +155,7 @@
     with jax.named_scope("project_theirs"):
         each_block(NB2, project_theirs)
 
+    partial_rest().start()
     cot_load.wait()
     ssr[...] = jnp.zeros_like(ssr)
     spr[...] = jnp.zeros_like(spr)
@@ -156,43 +170,64 @@
     with jax.named_scope("project_ours"):
         each_block(NB2, project_ours)
 
-    def add_theirs(b):
+    def add_theirs(b, rows):
+        a = att[b, rows] + precv[b, rows].astype(F32)
+        att[b, rows] = a
+        s = cot[rows, columns(b)].astype(F32) * gain_ref[columns(b)][None, :]
+        sq, pr = a * a, a * s
+        for k in range(CB // 128):
+            ssr[rows] += sq[:, k * 128 : (k + 1) * 128]
+            spr[rows] += pr[:, k * 128 : (k + 1) * 128]
+
+    def add_head(b):
         with jax.named_scope("wait_partial"):
             partial_send(b).wait_recv()
-        a = att[b] + precv[b].astype(F32)
-        att[b] = a
-        s = cot[:, columns(b)].astype(F32) * gain_ref[:, columns(b)]
-        sq, pr = a * a, a * s
-        for k in range(CB // 128):
-            ssr[...] += sq[:, k * 128 : (k + 1) * 128]
-            spr[...] += pr[:, k * 128 : (k + 1) * 128]
-
-    with jax.named_scope("add_theirs"):
-        each_block(NB2, add_theirs)
-
-    inverse = lax.rsqrt(jnp.sum(ssr[...], axis=1, keepdims=True) / D + norm_floor)
-    mean_sn = inverse * (jnp.sum(spr[...], axis=1, keepdims=True) / D)
-
-    def ga_send(h, j):
-        return send(gaf.at[h, j, m], gaf.at[h, j, m], ga_s.at[0], ga_r.at[j], "mp", om)
+        add_theirs(b, head)
+
+    with jax.named_scope("add_head"):
+        each_block(NB2, add_head)
+
+    def row_terms(rows):
+        inverse = lax.rsqrt(jnp.sum(ssr[rows], axis=1, keepdims=True) / D + norm_floor)
+        return inverse, inverse * (jnp.sum(spr[rows], axis=1, keepdims=True) / D)
+
+    def ga_send(j, rows):
+        part = gaf.at[:, j, m, rows]
+        return send(part, part, ga_s.at[0], ga_r.at[j], "mp", om)
 
     def side_send(j, who):
         return send(gaf.at[oc, j, who], gas.at[j, who], sa_s.at[0], sa_r.at[j], "dp_3", oc)
 
-    def norm_gradient(j):
+    def norm_gradient(j, rows, terms):
+        inverse, mean_sn = terms
         for h in range(2):
             b = h * NB + j
-            a = att[b]
-            u = cot[:, columns(b)].astype(F32)
-            s = u * gain_ref[:, columns(b)]
-            normed = a * inverse
-            gaf[h, j, m] = (inverse * (s - normed * mean_sn)).astype(BF16)
-            ga_send(h, j).start()
-            gz[z, pl.ds(b, 1), :] = jnp.sum(u * normed, axis=0, keepdims=True)
+            u = cot[rows, columns(b)].astype(F32)
+            s = u * gain_ref[columns(b)][None, :]
+            normed = att[b, rows] * inverse
+            gaf[h, j, m, rows] = (inverse * (s - normed * mean_sn)).astype(BF16)
+            gz[z, pl.ds(b, 1), :] += jnp.sum(u * normed, axis=0, keepdims=True)
+        ga_send(j, rows).start()
+
+    head_terms = row_terms(head)
+    with jax.named_scope("norm_head"):
+        each_block(AHEAD, lambda j: norm_gradient(j, head, head_terms))
+    with jax.named_scope("add_tail"):
+        partial_rest().wait_recv()
+        each_block(NB2, lambda b: add_theirs(b, tail))
+    tail_terms = row_terms(tail)
+
+    def norm_tail(j):
+        norm_gradient(j, tail, tail_terms)
         side_send(j, m).start()
 
-    with jax.named_scope("norm_gradient"):
-        each_block(NB, norm_gradient)
+    def norm_both(j):
+        norm_gradient(j, head, head_terms)
+        norm_tail(j)
+
+    with jax.named_scope("norm_tail"):
+        each_block(AHEAD, norm_tail)
+        each_block(NB - AHEAD, lambda j: norm_both(j + AHEAD))
 
     def gain_hop(buf, axis, me, n, ss, rs):
         return [
@@ -231,7 +266,7 @@
                 copy.start()
         else:
             for b in range(NB2):
-                gg_ref[:, b * CB : (b + 1) * CB] = total[b : b + 1, :]
+                gg_ref[b * CB : (b + 1) * CB] = total[b]
 
     ctx_swap().wait_recv()
 
@@ -239,23 +274,23 @@
         landed(gaf.at[:, j, om], ga_r.at[j])
         side_send(j, om).start()
 
-    def ring(j, buf, slot, n, me, axis, ss, rs):
+    def ring(j, out, buf, slot, n, me, axis, ss, rs):
         size, steps = NG // n, n // 2
         half = size // 2
 
-        def rows(t, k):
+        def target(t, k):
             far = steps + 1 - t
-            target = away(me, far if k == 0 else n - far, n)
+            return away(me, far if k == 0 else n - far, n) * size
+
+        def out_rows(t, k):
             if t == 1:
-                return pl.ds(target * size + k * half, half)
-            return pl.ds(target * size, size)
+                return pl.ds(k * half, half)
+            return pl.ds(size + (t - 2) * 2 * size + k * size, size)
 
         def hop(t, k):
             peer = away(me, 1 if k == 0 else n - 1, n)
             dst = buf.at[slot, t - 1, k, pl.ds(0, half)] if t == 1 else buf.at[slot, t - 1, k]
-            return send(
-                grad.at[j, rows(t, k)], dst, ss.at[slot], rs.at[slot, t - 1], axis, peer
-            )
+            return send(out.at[slot, out_rows(t, k)], dst, ss.at[slot], rs.at[slot, t - 1], axis, peer)
 
         def arrived(t, k):
             return (buf[slot, t - 1, k, :half] if t == 1 else buf[slot, t - 1, k]).astype(F32)
@@ -263,36 +298,43 @@
         def wait(t):
             landed(buf.at[slot, 0, :, pl.ds(0, half)] if t == 1 else buf.at[slot, t - 1], rs.at[slot, t - 1])
 
-        def start(t):
+        def start():
             for k in range(2):
-                hop(t, k).start()
+                out[slot, out_rows(1, k)] = grad[j, pl.ds(target(1, k) + k * half, half)].astype(BF16)
+            for k in range(2):
+                hop(1, k).start()
 
         def add_and_start(t):
             wait(t - 1)
             for k in range(2):
-                far = steps + 1 - t
-                target = away(me, far if k == 0 else n - far, n)
+                at = target(t, k)
                 if t == 2:
-                    part = pl.ds(target * size + k * half, half)
+                    base = size + k * size
+                    mine, other = k * half, (1 - k) * half
+                    total = grad[j, pl.ds(at + mine, half)] + arrived(1, k)
+                    out[slot, base + mine : base + mine + half] = total.astype(BF16)
+                    rest = grad[j, pl.ds(at + other, half)]
+                    out[slot, base + other : base + other + half] = rest.astype(BF16)
                 else:
-                    part = pl.ds(target * size, size)
-                grad[j, part] = (grad[j, part].astype(F32) + arrived(t - 1, k)).astype(BF16)
-            start(t)
+                    total = grad[j, pl.ds(at, size)] + arrived(t - 1, k)
+                    out[slot, out_rows(t, k)] = total.astype(BF16)
+            for k in range(2):
+                hop(t, k).start()
 
         def total():
             wait(steps)
-            return grad[j, pl.ds(me * size, size)].astype(F32) + arrived(steps, 0) + arrived(steps, 1)
+            return grad[j, pl.ds(me * size, size)] + arrived(steps, 0) + arrived(steps, 1)
 
         def sent():
-            landed(grad.at[j, pl.ds(0, (2 * steps - 1) * size)], ss.at[slot])
+            landed(out.at[slot], ss.at[slot])
 
         return start, add_and_start, total, sent
 
     def x_ring(j):
-        return ring(j, rx, j, NX, x, "dp_2", x_s, x_r)
+        return ring(j, ox, rx, j, NX, x, "dp_2", x_s, x_r)
 
     def z_ring(i):
-        return ring(ZB[i], rz, i, NZ, z, "dp_0", zz_s, zz_r)
+        return ring(ZB[i], oz, rz, i, NZ, z, "dp_0", zz_s, zz_r)
 
     def z_send(j, d, e):
         zp, yp = away(z, d, NZ), away(yl, e, NY)
@@ -317,7 +359,6 @@
             cols = slice(q * QR, (q + 1) * QR)
             part = dot_tn(ctx_o[:, :, cols].reshape(T, QR), ours)
             part = part + dot_tn(ctx_s[:, :, cols].reshape(T, QR), theirs)
-            part = part.astype(BF16)
             if z_first:
                 grad[j, q * per : (q + 1) * per] = part.reshape(per, 16, CB)
             else:
@@ -328,28 +369,32 @@
 
     def x_start(j):
         weight_grad(j, False)
-        x_ring(j)[0](1)
+        x_ring(j)[0]()
 
     def x_first(j):
         x_ring(j)[1](2)
 
     def x_second(j):
-        zs[j] = x_ring(j)[2]().astype(BF16).reshape(NZ, NY, 16, CB)
+        total = x_ring(j)[2]()
+        own[j] = total
+        zs[j] = total.astype(BF16).reshape(NZ, NY, 16, CB)
         for d, e in owners:
             z_send(j, d, e).start()
 
     def z_start(i):
         weight_grad(ZB[i], True)
-        z_ring(i)[0](1)
+        z_ring(i)[0]()
 
     def z_last(i):
-        xs[i] = z_ring(i)[2]().astype(BF16).reshape(NY, NX, 16, CB)
+        total = z_ring(i)[2]()
+        own[ZB[i], : NY * NX] = total
+        xs[i] = total.astype(BF16).reshape(NY, NX, 16, CB)
         for d, e in x_owners:
             xo_send(i, d, e).start()
 
     def x_sum(i):
         landed(xr.at[i, pl.ds(1, NX * NY - 1)], xo_r.at[i])
-        total = xs[i, yl, x].astype(F32)
+        total = own[ZB[i], yl * NX + x]
         for d, e in x_owners:
             total = total + xr[i, d * NY + e].astype(F32)
         to_core(ZB[i], total)
@@ -372,7 +417,7 @@
 
     def z_sum(j):
         landed(zr.at[j, pl.ds(1, ZY - 1)], z_r.at[j])
-        total = zs[j, z, yl].astype(F32)
+        total = own[j, z * NY + yl]
         for d, e in owners:
             total = total + zr[j, d * NY + e].astype(F32)
         to_core(j, total)
@@ -393,12 +438,11 @@
 
     steps_z = NZ // 2
     stages = [(x_start, 1), (x_first, 2), (x_second, 4), (z_sum, 6)]
-    z_stages = [(z_start, Z_LAGS[0])]
-    for n in range(2, steps_z + 1):
-        z_stages.append((lambda i, n=n: z_ring(i)[1](n), Z_LAGS[n - 1]))
-    z_stages += [(z_last, Z_LAGS[steps_z]), (x_sum, Z_LAGS[steps_z + 1])]
-    gain_steps = (2, 4, NB + 1, NB + 2, NB + 3)
-    last = max(NB + 6, max(ZB) + Z_LAGS[steps_z + 1] + 1)
+    z_stages = [z_start]
+    z_stages += [lambda i, n=n: z_ring(i)[1](n) for n in range(2, steps_z + 1)]
+    z_stages += [z_last, x_sum]
+    gain_steps = (2, 4, NB, NB + 3, NB + 5)
+    last = max([NB + 6] + [b + Z_PLAN[b][steps_z + 1] + 1 for b in ZB])
 
     def step(t):
         for stage, lag in stages:
@@ -411,12 +455,12 @@
                 with jax.named_scope(stage.__name__):
                     stage(t - lag)
 
-        for stage, lag in z_stages:
+        for n, stage in enumerate(z_stages):
             for i, b in enumerate(ZB):
 
-                @pl.when(t == b + lag)
+                @pl.when(t == b + Z_PLAN[b][n])
                 def _():
-                    with jax.named_scope(f"z{lag}"):
+                    with jax.named_scope(f"z{n}#b={b}"):
                         stage(i)
 
         @pl.when(t < NB)
@@ -530,7 +574,7 @@
         pltpu.VMEM((8, D), BF16),
         pltpu.VMEM((8, D), F32),
         pltpu.VMEM((8, D), F32),
-        pltpu.VMEM((1, D), F32),
+        pltpu.VMEM((D,), F32),
         pltpu.VMEM((H // QR, T, QR), BF16),
         pltpu.VMEM((2, TH, H), BF16),
         pltpu.VMEM((2, TH, H), BF16),
@@ -543,7 +587,10 @@
         pltpu.VMEM((TH, 128), F32),
         pltpu.VMEM((2, NB, 2, TH, CB), BF16),
         pltpu.VMEM((NB, 2, TH, CB), BF16),
-        pltpu.VMEM((NB, NZ * NY * NX, 16, CB), BF16),
+        pltpu.VMEM((NB, NZ * NY * NX, 16, CB), F32),
+        pltpu.VMEM((NB, max(ZY, NY * NX), 16, CB), F32),
+        pltpu.VMEM((NB, (NX - 1) * ZY, 16, CB), BF16),
+        pltpu.VMEM((NZB, (NZ - 1) * NY * NX, 16, CB), BF16),
         pltpu.VMEM((NB, NX // 2, 2, ZY, 16, CB), BF16),
         pltpu.VMEM((NZB, NZ // 2, 2, NY * NX, 16, CB), BF16),
         pltpu.VMEM((NB, NZ, NY, 16, CB), BF16),
@@ -560,7 +607,7 @@
         pltpu.VMEM((2, rows8, CB), F32),
         pltpu.VMEM((2, rows8, CB), F32),
         dma((NB2,)), dma((5,)), dma((2,)),
-        dma((1,)), dma((NB2,)),
+        dma((1,)), dma((NB2 + 1,)),
         dma((1,)), dma((NB,)),
         dma((1,)), dma((NB,)),
         dma((NB,)), dma((NB, NX // 2)),
@@ -579,7 +626,7 @@
             jax.ShapeDtypeStruct((8, D), BF16),
             jax.ShapeDtypeStruct((8, D), F32),
             jax.ShapeDtypeStruct((8, D), F32),
-            jax.ShapeDtypeStruct((1, D), F32),
+            jax.ShapeDtypeStruct((D,), F32),
             jax.ShapeDtypeStruct((T, H), BF16),
         ],
         in_specs=[any_space, any_space, any_space, vmem, any_space, any_space],
@@ -589,9 +636,9 @@
             collective_id=0, has_side_effects=True, vmem_limit_bytes=60 * 1024 * 1024
         ),
         name="step",
-    )(context, out_weight, cotangent, norm_gain.reshape(1, D), first_moment[0], second_moment[0])
+    )(context, out_weight, cotangent, norm_gain, first_moment[0], second_moment[0])
     nw, n1, n2, gg, gc = delivered(results)
-    return (nw[None], n1[None], n2[None], gg.reshape(D), gc)
+    return (nw[None], n1[None], n2[None], gg, gc)
 
 
 def build(finer, block):

time: 93.7 us -> 89.5 us (0.955)
  other arithmetic: 1.36 us -> 0 us
  local copies, waits for them, and re-layouts: 1.33 us -> 0 us
  Pallas kernels: 90 us -> 88.7 us
    pallas_call x1 -> x0, other arithmetic: 1.36 us -> none  [delivered(): pl.pallas_call(deliver, out_shape=[jax.ShapeDtypeStruct(a.shape, a.dtype)...]
    reshape x1 -> x0, local copies, waits for them, and re-layouts: 1.33 us -> none  [per_device(): norm_gain.reshape(1, D)]
    pallas_call x1, Pallas kernels: 87.8 us -> 86.5 us  [per_device(): pl.pallas_call(functools.partial(kernel, dims), out_shape=[jax.ShapeDtype...]
where the time goes in v4:
time: 89.5 us; the launch traced here: 89.3 us
  Pallas kernels  88.7 us (99%)
    pallas_call x1, Pallas kernels, per_device(): pl.pallas_call(functools.partial(kernel, dims), out_shape=[jax.ShapeDtype...  86.5 us
    pallas_call x1, Pallas kernels, delivered(): pl.pallas_call(deliver, out_shape=[jax.ShapeDtypeStruct(a.shape, a.dtype)...  2.18 us

profile of v4, /device:TPU:1, one launch (start us, length us, event | category | flops | bytes accessed | tf_op | source)
XLA Modules:
  0.0 89.3 jit_solution(12052905099925962419)
XLA Ops:
  0.6 86.5 %step.1 = (bf16[8,3584]{1,0:T(8,128)(2,1)}, f32[8,3584]{1,0:T(8,128)}, f32[8,3584]{1,0:T(8,128)}, f32[3584]{0:T(1024)}, bf16[320,1024]{1,0:T(8,128)(2,1)}) custom-call(bf16[320,1024]{1,0:T(8,128)(2,1)} %ctx_hbm.1, bf16[1024,3584]{1,0:T(8,128)(2,1)} %w_hbm.1, bf16[320,3584]{1,0:T(8,128)(2,1)} %cot_hbm.1, f32[3584]{0:T(1024)} %gain_ref.1, f32[8,3584]{1,0:T(8,128)} %bitcast.5, ...), custom_call_target="tpu_custom_call" | custom-call | tf_op jit(solution)/shard_map/step/pallas_call | solution.py:623
  87.2 2.2 %deliver.1 = (bf16[8,3584]{1,0:T(8,128)(2,1)}, f32[8,3584]{1,0:T(8,128)}, f32[8,3584]{1,0:T(8,128)}, f32[3584]{0:T(1024)}, bf16[320,1024]{1,0:T(8,128)(2,1)}) custom-call(bf16[8,3584]{1,0:T(8,128)(2,1)} %get-tuple-element.15.refs_0_, f32[8,3584]{1,0:T(8,128)} %get-tuple-element.16.refs_1_, f32[8,3584]{1,0:T(8,128)} %get-tuple-element.17.refs_2_, ...), custom_call_target="tpu_custom_call" | custom-call | tf_op jit(solution)/shard_map/deliver/pallas_call | solution.py:550

commit v5 on v4

--- a/solution.py
+++ b/solution.py
@@ -22,7 +22,7 @@
 QR = 256
 
 
-Z_PLAN = {0: (1, 2, 4, 6, 8, 10), 1: (1, 2, 4, 6, 8, 9), 3: (1, 2, 4, 5, 7, 9)}
+Z_PLAN = {0: (0, 1, 3, 5, 7, 9), 1: (0, 1, 3, 5, 7, 8), 3: (0, 1, 3, 4, 6, 8)}
 
 
 AHEAD = 2
@@ -67,11 +67,11 @@
     dims,
     ctx_hbm, w_hbm, cot_hbm, gain_ref, m1_hbm, m2_hbm,
     nw_hbm, n1_hbm, n2_hbm, gg_hbm, gc_hbm,
-    nw_ref, n1_ref, n2_ref, gg_ref, gcv,
+    nw_ref, n1_ref, n2_ref, gg_ref, gcv, gcs, gcr, gcb,
     ctx_o, ctx_s, wv, cot, att, psend, precv, ssr, spr, gaf, gas,
     grad, own, ox, oz, rx, rz, zs, zr, xs, xr, fs, gr, m1v, m2v, gz, gx, gy, gm, gk,
     ld_w, ld, c_sem, p_s, p_r, ga_s, ga_r, sa_s, sa_r, x_s, x_r, zz_s, zz_r,
-    z_s, z_r, xo_s, xo_r, o_sem, f_s, f_r, gt_s, gt_r,
+    z_s, z_r, xo_s, xo_r, o_sem, f_s, f_r, gt_s, gt_r, gc_s,
 ):
     NZ, NY, NX, TH, H, D, NB, CB = dims
     ZB = z_blocks(NB)
@@ -122,7 +122,7 @@
     m2_load.start()
 
     barrier = pltpu.get_barrier_semaphore()
-    peers = [{"dp_3": oc}, {"mp": om}]
+    peers = [{"dp_3": oc}, {"mp": om}, {"mp": om, "dp_3": oc}]
     peers += [{"dp_2": away(x, d, NX), "dp_1": away(yl, e, NY)} for d, e in x_owners if d]
     peers += [{"dp_0": away(z, d, NZ), "dp_1": away(yl, e, NY)} for d, e in owners]
     for peer in peers:
@@ -191,12 +191,21 @@
         inverse = lax.rsqrt(jnp.sum(ssr[rows], axis=1, keepdims=True) / D + norm_floor)
         return inverse, inverse * (jnp.sum(spr[rows], axis=1, keepdims=True) / D)
 
-    def ga_send(j, rows):
-        part = gaf.at[:, j, m, rows]
-        return send(part, part, ga_s.at[0], ga_r.at[j], "mp", om)
-
-    def side_send(j, who):
-        return send(gaf.at[oc, j, who], gas.at[j, who], sa_s.at[0], sa_r.at[j], "dp_3", oc)
+    def ga_sends(j, rows):
+        here, there = gaf.at[c, j, m, rows], gaf.at[oc, j, m, rows]
+        straight = send(here, here, ga_s.at[0], ga_r.at[j], "mp", om)
+        crossed = pltpu.make_async_remote_copy(
+            src_ref=there,
+            dst_ref=gas.at[j, m, rows],
+            send_sem=ga_s.at[0],
+            recv_sem=sa_r.at[j],
+            device_id={"mp": om, "dp_3": oc},
+            device_id_type=MESH,
+        )
+        return straight, crossed
+
+    def side_send(j):
+        return send(gaf.at[oc, j, m], gas.at[j, m], sa_s.at[0], sa_r.at[j], "dp_3", oc)
 
     def norm_gradient(j, rows, terms):
         inverse, mean_sn = terms
@@ -207,7 +216,8 @@
             normed = att[b, rows] * inverse
             gaf[h, j, m, rows] = (inverse * (s - normed * mean_sn)).astype(BF16)
             gz[z, pl.ds(b, 1), :] += jnp.sum(u * normed, axis=0, keepdims=True)
-        ga_send(j, rows).start()
+        for copy in ga_sends(j, rows):
+            copy.start()
 
     head_terms = row_terms(head)
     with jax.named_scope("norm_head"):
@@ -219,7 +229,7 @@
 
     def norm_tail(j):
         norm_gradient(j, tail, tail_terms)
-        side_send(j, m).start()
+        side_send(j).start()
 
     def norm_both(j):
         norm_gradient(j, head, head_terms)
@@ -269,10 +279,6 @@
                 gg_ref[b * CB : (b + 1) * CB] = total[b]
 
     ctx_swap().wait_recv()
-
-    def gather_grad_attn(j):
-        landed(gaf.at[:, j, om], ga_r.at[j])
-        side_send(j, om).start()
 
     def ring(j, out, buf, slot, n, me, axis, ss, rs):
         size, steps = NG // n, n // 2
@@ -351,6 +357,7 @@
         return send(fs.at[oc, j], gr.at[c, j], f_s.at[0], f_r.at[0], "dp_3", oc)
 
     def weight_grad(j, z_first):
+        landed(gaf.at[c, j, om], ga_r.at[j])
         landed(gas.at[j], sa_r.at[j])
         ours = gaf[c, j].reshape(T, CB)
         theirs = gas[j].reshape(T, CB)
@@ -422,27 +429,46 @@
             total = total + zr[j, d * NY + e].astype(F32)
         to_core(j, total)
 
-    def context_out(k):
-        rows = pl.ds(pl.multiple_of(k * QR, QR), QR)
-        return pltpu.make_async_copy(gcv.at[k], gc_hbm.at[:, rows], o_sem.at[4])
-
-    def context_grad(k):
+    def context_swap(k):
+        return send(gcs.at[k], gcr.at[k], gc_s.at[0], gc_s.at[1], "dp_3", oc)
+
+    def context_dots(k, blocks):
         rows = pl.ds(pl.multiple_of(k * QR, QR), QR)
         total = None
-        for h in range(2):
-            for j in range(NB):
-                term = dot_nt(gaf[h, j].reshape(T, CB), wv[h * NB + j, rows, :])
-                total = term if total is None else total + term
-        gcv[k] = total.astype(BF16)
-        context_out(k).start()
+        for left_hand, b in blocks:
+            term = dot_nt(left_hand, wv[b, rows, :])
+            total = term if total is None else total + term
+        return total
+
+    def context_own(k):
+        own_blocks = [(gaf[h, j, m], h * NB + j) for h in range(2) for j in range(NB)]
+        gcv[k, m] = context_dots(k, own_blocks).astype(BF16)
+
+    def context_grad(k):
+        gcs[k] = context_dots(k, [(gas[j, om], c * NB + j) for j in range(NB)])
+        context_swap(k).start()
+        gcb[k] = context_dots(k, [(gaf[c, j, om], c * NB + j) for j in range(NB)])
+
+    def context_join():
+        landed(gcr, gc_s.at[1])
+        for k in range(H // QR):
+            gcv[k, om] = (gcb[k] + gcr[k]).astype(BF16)
+            for who in range(2):
+                pltpu.make_async_copy(
+                    gcv.at[k, who],
+                    gc_hbm.at[pl.ds(who * TH, TH), pl.ds(k * QR, QR)],
+                    o_sem.at[4],
+                ).start()
 
     steps_z = NZ // 2
-    stages = [(x_start, 1), (x_first, 2), (x_second, 4), (z_sum, 6)]
+    NK = H // QR
+    per = max(1, NK // 2)
+    stages = [(x_start, 0), (z_sum, 5), (x_second, 3), (x_first, 1)]
     z_stages = [z_start]
     z_stages += [lambda i, n=n: z_ring(i)[1](n) for n in range(2, steps_z + 1)]
     z_stages += [z_last, x_sum]
-    gain_steps = (2, 4, NB, NB + 3, NB + 5)
-    last = max([NB + 6] + [b + Z_PLAN[b][steps_z + 1] + 1 for b in ZB])
+    gain_steps = (2, 3, NB - 1, NB + 2, NB + 4)
+    last = max([NB + 5] + [b + Z_PLAN[b][steps_z + 1] + 1 for b in ZB])
 
     def step(t):
         for stage, lag in stages:
@@ -463,11 +489,6 @@
                     with jax.named_scope(f"z{n}#b={b}"):
                         stage(i)
 
-        @pl.when(t < NB)
-        def _():
-            with jax.named_scope("gather"):
-                gather_grad_attn(t)
-
         for k, when in enumerate(gain_steps):
 
             @pl.when(t == when)
@@ -475,11 +496,18 @@
                 with jax.named_scope("gain_stage"):
                     gain_stage(k)
 
-        @pl.when((t >= NB) & (t < NB + H // QR))
+        @pl.when((t >= NB) & (t < NB + NK // per))
         def _():
             with jax.named_scope("context_grad"):
-                context_grad(t - NB)
-
+                each_block(per, lambda i: context_grad((t - NB) * per + i))
+
+        @pl.when(t == NB + 2)
+        def _():
+            with jax.named_scope("context_join"):
+                context_join()
+
+    with jax.named_scope("context_own"):
+        each_block(NK, context_own)
     each_block(last, step)
 
     gr[c] = fs[c]
@@ -513,7 +541,8 @@
             landed(hop[0].at[pl.ds(0, hop[3] - 1)], hop[4])
 
     landed(gaf.at[:, :, m], ga_s.at[0])
-    landed(gas, sa_s.at[0])
+    landed(gaf.at[0, :, m], sa_s.at[0])
+    landed(gcs, gc_s.at[0])
     landed(fs.at[oc], f_s.at[0])
 
     def drain(j):
@@ -575,7 +604,10 @@
         pltpu.VMEM((8, D), F32),
         pltpu.VMEM((8, D), F32),
         pltpu.VMEM((D,), F32),
-        pltpu.VMEM((H // QR, T, QR), BF16),
+        pltpu.VMEM((H // QR, 2, TH, QR), BF16),
+        pltpu.VMEM((H // QR, TH, QR), F32),
+        pltpu.VMEM((H // QR, TH, QR), F32),
+        pltpu.VMEM((H // QR, TH, QR), F32),
         pltpu.VMEM((2, TH, H), BF16),
         pltpu.VMEM((2, TH, H), BF16),
         pltpu.VMEM((NB2, H, CB), BF16),
@@ -617,6 +649,7 @@
         dma((5,)),
         dma((1,)), dma((1,)),
         dma((5,)), dma((5,)),
+        dma((2,)),
     ]
     any_space = pl.BlockSpec(memory_space=pl.ANY)
     vmem = pl.BlockSpec(memory_space=pltpu.VMEM)

time: 89.5 us -> 88.2 us (0.985)
  Pallas kernels: 88.7 us -> 87.4 us
    pallas_call x1, Pallas kernels: 86.5 us -> 85.2 us  [per_device(): pl.pallas_call(functools.partial(kernel, dims), out_shape=[jax.ShapeDtype...]
where the time goes in v5:
time: 88.2 us; the launch traced here: 88 us
  Pallas kernels  87.4 us (99%)
    pallas_call x1, Pallas kernels, per_device(): pl.pallas_call(functools.partial(kernel, dims), out_shape=[jax.ShapeDtype...  85.2 us
    pallas_call x1, Pallas kernels, delivered(): pl.pallas_call(deliver, out_shape=[jax.ShapeDtypeStruct(a.shape, a.dtype)...  2.18 us

profile of v5, /device:TPU:1, one launch (start us, length us, event | category | flops | bytes accessed | tf_op | source)
XLA Modules:
  0.0 88.0 jit_solution(8579987361976907972)
XLA Ops:
  0.6 85.2 %step.1 = (bf16[8,3584]{1,0:T(8,128)(2,1)}, f32[8,3584]{1,0:T(8,128)}, f32[8,3584]{1,0:T(8,128)}, f32[3584]{0:T(1024)}, bf16[320,1024]{1,0:T(8,128)(2,1)}) custom-call(bf16[320,1024]{1,0:T(8,128)(2,1)} %ctx_hbm.1, bf16[1024,3584]{1,0:T(8,128)(2,1)} %w_hbm.1, bf16[320,3584]{1,0:T(8,128)(2,1)} %cot_hbm.1, f32[3584]{0:T(1024)} %gain_ref.1, f32[8,3584]{1,0:T(8,128)} %bitcast.5, ...), custom_call_target="tpu_custom_call" | custom-call | tf_op jit(solution)/shard_map/step/pallas_call | solution.py:656
  85.9 2.2 %deliver.1 = (bf16[8,3584]{1,0:T(8,128)(2,1)}, f32[8,3584]{1,0:T(8,128)}, f32[8,3584]{1,0:T(8,128)}, f32[3584]{0:T(1024)}, bf16[320,1024]{1,0:T(8,128)(2,1)}) custom-call(bf16[8,3584]{1,0:T(8,128)(2,1)} %get-tuple-element.15.refs_0_, f32[8,3584]{1,0:T(8,128)} %get-tuple-element.16.refs_1_, f32[8,3584]{1,0:T(8,128)} %get-tuple-element.17.refs_2_, ...), custom_call_target="tpu_custom_call" | custom-call | tf_op jit(solution)/shard_map/deliver/pallas_call | solution.py:579

commit v6 on v5

--- a/solution.py
+++ b/solution.py
@@ -22,7 +22,7 @@
 QR = 256
 
 
-Z_PLAN = {0: (0, 1, 3, 5, 7, 9), 1: (0, 1, 3, 5, 7, 8), 3: (0, 1, 3, 4, 6, 8)}
+Z_PLAN = {0: (0, 1, 3, 5, 7, 9), 1: (0, 1, 3, 5, 7, 9), 3: (0, 1, 2, 3, 5, 7)}
 
 
 AHEAD = 2
@@ -65,11 +65,11 @@
 
 def kernel(
     dims,
-    ctx_hbm, w_hbm, cot_hbm, gain_ref, m1_hbm, m2_hbm,
-    nw_hbm, n1_hbm, n2_hbm, gg_hbm, gc_hbm,
-    nw_ref, n1_ref, n2_ref, gg_ref, gcv, gcs, gcr, gcb,
+    ctx_hbm, w_hbm, cot_hbm, gain_ref,
+    g_hbm, gg_hbm, gc_hbm,
+    gg_ref, gcv, gcs, gcr, gcb,
     ctx_o, ctx_s, wv, cot, att, psend, precv, ssr, spr, gaf, gas,
-    grad, own, ox, oz, rx, rz, zs, zr, xs, xr, fs, gr, m1v, m2v, gz, gx, gy, gm, gk,
+    grad, own, ox, oz, rx, rz, zs, zr, xs, xr, fs, gz, gx, gy, gm, gk,
     ld_w, ld, c_sem, p_s, p_r, ga_s, ga_r, sa_s, sa_r, x_s, x_r, zz_s, zz_r,
     z_s, z_r, xo_s, xo_r, o_sem, f_s, f_r, gt_s, gt_r, gc_s,
 ):
@@ -100,14 +100,18 @@
 
         lax.fori_loop(0, n, step, 0)
 
+    barrier = pltpu.get_barrier_semaphore()
+    peers = [{"dp_3": oc}, {"mp": om}, {"mp": om, "dp_3": oc}]
+    peers += [{"dp_2": away(x, d, NX), "dp_1": away(yl, e, NY)} for d, e in x_owners if d]
+    peers += [{"dp_0": away(z, d, NZ), "dp_1": away(yl, e, NY)} for d, e in owners]
+    for peer in peers:
+        pl.semaphore_signal(barrier, inc=1, device_id=peer, device_id_type=MESH)
     ctx_loads = [
         pltpu.make_async_copy(ctx_hbm.at[pl.ds(k * TH, TH), :], ctx_o.at[k], ld.at[k]) for k in range(2)
     ]
     cot_load = pltpu.make_async_copy(
         cot_hbm.at[pl.ds(pl.multiple_of(m * TH, TH), TH), :], cot, ld.at[2]
     )
-    m1_load = pltpu.make_async_copy(m1_hbm, m1v, ld.at[3])
-    m2_load = pltpu.make_async_copy(m2_hbm, m2v, ld.at[4])
 
     def w_load(b):
         return pltpu.make_async_copy(
@@ -118,15 +122,7 @@
         copy.start()
     each_block(NB2, lambda b: w_load(b).start())
     cot_load.start()
-    m1_load.start()
-    m2_load.start()
-
-    barrier = pltpu.get_barrier_semaphore()
-    peers = [{"dp_3": oc}, {"mp": om}, {"mp": om, "dp_3": oc}]
-    peers += [{"dp_2": away(x, d, NX), "dp_1": away(yl, e, NY)} for d, e in x_owners if d]
-    peers += [{"dp_0": away(z, d, NZ), "dp_1": away(yl, e, NY)} for d, e in owners]
-    for peer in peers:
-        pl.semaphore_signal(barrier, inc=1, device_id=peer, device_id_type=MESH)
+
     with jax.named_scope("greet"):
         pl.semaphore_wait(barrier, len(peers))
 
@@ -280,13 +276,13 @@
 
     ctx_swap().wait_recv()
 
-    def ring(j, out, buf, slot, n, me, axis, ss, rs):
-        size, steps = NG // n, n // 2
+    def ring(j, out, buf, n, me, axis, ss, rs, size, stride, base):
+        steps = n // 2
         half = size // 2
 
         def target(t, k):
             far = steps + 1 - t
-            return away(me, far if k == 0 else n - far, n) * size
+            return away(me, far if k == 0 else n - far, n) * stride + base
 
         def out_rows(t, k):
             if t == 1:
@@ -295,18 +291,18 @@
 
         def hop(t, k):
             peer = away(me, 1 if k == 0 else n - 1, n)
-            dst = buf.at[slot, t - 1, k, pl.ds(0, half)] if t == 1 else buf.at[slot, t - 1, k]
-            return send(out.at[slot, out_rows(t, k)], dst, ss.at[slot], rs.at[slot, t - 1], axis, peer)
+            dst = buf(t - 1, k, pl.ds(0, half)) if t == 1 else buf(t - 1, k, pl.ds(0, size))
+            return send(out(out_rows(t, k)), dst, ss, rs(t - 1), axis, peer)
 
         def arrived(t, k):
-            return (buf[slot, t - 1, k, :half] if t == 1 else buf[slot, t - 1, k]).astype(F32)
+            return buf(t - 1, k, pl.ds(0, half if t == 1 else size))[...].astype(F32)
 
         def wait(t):
-            landed(buf.at[slot, 0, :, pl.ds(0, half)] if t == 1 else buf.at[slot, t - 1], rs.at[slot, t - 1])
+            landed(buf(t - 1, slice(None), pl.ds(0, half if t == 1 else size)), rs(t - 1))
 
         def start():
             for k in range(2):
-                out[slot, out_rows(1, k)] = grad[j, pl.ds(target(1, k) + k * half, half)].astype(BF16)
+                out(out_rows(1, k))[...] = grad[j, pl.ds(target(1, k) + k * half, half)].astype(BF16)
             for k in range(2):
                 hop(1, k).start()
 
@@ -315,37 +311,48 @@
             for k in range(2):
                 at = target(t, k)
                 if t == 2:
-                    base = size + k * size
+                    at_out = size + k * size
                     mine, other = k * half, (1 - k) * half
                     total = grad[j, pl.ds(at + mine, half)] + arrived(1, k)
-                    out[slot, base + mine : base + mine + half] = total.astype(BF16)
+                    out(pl.ds(at_out + mine, half))[...] = total.astype(BF16)
                     rest = grad[j, pl.ds(at + other, half)]
-                    out[slot, base + other : base + other + half] = rest.astype(BF16)
+                    out(pl.ds(at_out + other, half))[...] = rest.astype(BF16)
                 else:
                     total = grad[j, pl.ds(at, size)] + arrived(t - 1, k)
-                    out[slot, out_rows(t, k)] = total.astype(BF16)
+                    out(out_rows(t, k))[...] = total.astype(BF16)
             for k in range(2):
                 hop(t, k).start()
 
         def total():
             wait(steps)
-            return grad[j, pl.ds(me * size, size)] + arrived(steps, 0) + arrived(steps, 1)
+            return grad[j, pl.ds(me * stride + base, size)] + arrived(steps, 0) + arrived(steps, 1)
 
         def sent():
-            landed(out.at[slot], ss.at[slot])
+            landed(out(pl.ds(0, (2 * steps - 1) * size)), ss)
 
         return start, add_and_start, total, sent
 
-    def x_ring(j):
-        return ring(j, ox, rx, j, NX, x, "dp_2", x_s, x_r)
+    def x_ring(j, r):
+        at = (1 - yl if r == 0 else yl) * NZ
+        return ring(
+            j,
+            lambda rows: ox.at[j, r, rows],
+            lambda t, k, rows: rx.at[j, r, t, k, rows],
+            NX, x, "dp_2", x_s.at[j, r], lambda t: x_r.at[j, r, t], NZ, ZY, at,
+        )
 
     def z_ring(i):
-        return ring(ZB[i], oz, rz, i, NZ, z, "dp_0", zz_s, zz_r)
+        return ring(
+            ZB[i],
+            lambda rows: oz.at[i, rows],
+            lambda t, k, rows: rz.at[i, t, k, rows],
+            NZ, z, "dp_0", zz_s.at[i], lambda t: zz_r.at[i, t], NX * NY, NX * NY, 0,
+        )
 
     def z_send(j, d, e):
         zp, yp = away(z, d, NZ), away(yl, e, NY)
         return pltpu.make_async_remote_copy(
-            src_ref=zs.at[j, zp, yp],
+            src_ref=zs.at[j, yp, zp],
             dst_ref=zr.at[j, d * NY + e],
             send_sem=z_s.at[j],
             recv_sem=z_r.at[j],
@@ -354,7 +361,7 @@
         )
 
     def core_send(j):
-        return send(fs.at[oc, j], gr.at[c, j], f_s.at[0], f_r.at[0], "dp_3", oc)
+        return send(fs.at[oc, j], g_hbm.at[c, j], f_s.at[0], f_r.at[0], "dp_3", oc)
 
     def weight_grad(j, z_first):
         landed(gaf.at[c, j, om], ga_r.at[j])
@@ -369,24 +376,31 @@
             if z_first:
                 grad[j, q * per : (q + 1) * per] = part.reshape(per, 16, CB)
             else:
-                part = part.reshape(per // NX, NX, 16, CB)
+                zq = per // (NX * NY)
+                part = part.reshape(zq, NY, NX, 16, CB)
                 for k in range(NX):
-                    at = k * ZY + q * (per // NX)
-                    grad[j, at : at + per // NX] = part[:, k]
+                    for e in range(NY):
+                        at = k * ZY + e * NZ + q * zq
+                        grad[j, at : at + zq] = part[:, e, k]
 
     def x_start(j):
         weight_grad(j, False)
-        x_ring(j)[0]()
+        for r in range(2):
+            x_ring(j, r)[0]()
 
     def x_first(j):
-        x_ring(j)[1](2)
+        for r in range(2):
+            x_ring(j, r)[1](2)
 
     def x_second(j):
-        total = x_ring(j)[2]()
-        own[j] = total
-        zs[j] = total.astype(BF16).reshape(NZ, NY, 16, CB)
-        for d, e in owners:
-            z_send(j, d, e).start()
+        for r in range(2):
+            side = 1 - yl if r == 0 else yl
+            total = x_ring(j, r)[2]()
+            own[j, pl.ds(side * NZ, NZ)] = total
+            zs[j, side] = total.astype(BF16)
+            for d, e in owners:
+                if (e == 0) == (r == 1):
+                    z_send(j, d, e).start()
 
     def z_start(i):
         weight_grad(ZB[i], True)
@@ -410,6 +424,7 @@
         fs[0, j] = total[:8]
         fs[1, j] = total[8:]
         core_send(j).start()
+        pltpu.make_async_copy(fs.at[c, j], g_hbm.at[c, j], o_sem.at[1]).start()
 
     def xo_send(i, d, e):
         xp, yp = away(x, d, NX), away(yl, e, NY)
@@ -424,7 +439,7 @@
 
     def z_sum(j):
         landed(zr.at[j, pl.ds(1, ZY - 1)], z_r.at[j])
-        total = own[j, z * NY + yl]
+        total = own[j, yl * NZ + z]
         for d, e in owners:
             total = total + zr[j, d * NY + e].astype(F32)
         to_core(j, total)
@@ -463,16 +478,18 @@
     steps_z = NZ // 2
     NK = H // QR
     per = max(1, NK // 2)
-    stages = [(x_start, 0), (z_sum, 5), (x_second, 3), (x_first, 1)]
+    stages = [(x_start, 0), (z_sum, 6), (x_second, 3), (x_first, 1)]
     z_stages = [z_start]
     z_stages += [lambda i, n=n: z_ring(i)[1](n) for n in range(2, steps_z + 1)]
     z_stages += [z_last, x_sum]
-    gain_steps = (2, 3, NB - 1, NB + 2, NB + 4)
-    last = max([NB + 5] + [b + Z_PLAN[b][steps_z + 1] + 1 for b in ZB])
+    gain_steps = (2, 3, NB - 1, NB + 2, NB + 5)
+    last = max([NB + 6] + [b + Z_PLAN[b][steps_z + 1] + 1 for b in ZB])
 
     def step(t):
         for stage, lag in stages:
             mine = (t >= lag) & (t < NB + lag)
+            if stage is x_second:
+                mine = mine & (t != NB - 1 + lag)
             for b in ZB:
                 mine = mine & (t != b + lag)
 
@@ -481,6 +498,11 @@
                 with jax.named_scope(stage.__name__):
                     stage(t - lag)
 
+        @pl.when(t == NB + 1)
+        def _():
+            with jax.named_scope("x_second_last"):
+                x_second(NB - 1)
+
         for n, stage in enumerate(z_stages):
             for i, b in enumerate(ZB):
 
@@ -510,29 +532,10 @@
         each_block(NK, context_own)
     each_block(last, step)
 
-    gr[c] = fs[c]
-    m1_load.wait()
-    m2_load.wait()
+    gain_out = pltpu.make_async_copy(gg_ref, gg_hbm, o_sem.at[0])
+    gain_out.start()
     with jax.named_scope("core_wait"):
-        landed(gr.at[oc], f_r.at[0])
-    row = pl.multiple_of(((z * NY + yl) * NX + x) * 16, 16)
-    for b in range(NB2):
-        cols = slice(b * CB, (b + 1) * CB)
-        g = gr[b // NB, b % NB]
-        first = beta_one * m1v[:, cols] + (1.0 - beta_one) * g
-        second = beta_two * m2v[:, cols] + (1.0 - beta_two) * g * g
-        both = wv[b, pl.ds(row, 16), :].astype(F32)
-        master = jnp.where(c == 0, both[:8], both[8:])
-        n1_ref[:, cols] = first
-        n2_ref[:, cols] = second
-        nw_ref[:, cols] = (master - learn_rate * first / (jnp.sqrt(second) + adam_floor)).astype(BF16)
-
-    outs = [
-        pltpu.make_async_copy(a, b, o_sem.at[i])
-        for i, (a, b) in enumerate([(nw_ref, nw_hbm), (n1_ref, n1_hbm), (n2_ref, n2_hbm), (gg_ref, gg_hbm)])
-    ]
-    for copy in outs:
-        copy.start()
+        landed(g_hbm.at[oc], f_r.at[0])
 
     ctx_swap().wait_send()
     landed(psend, p_s.at[0])
@@ -546,7 +549,8 @@
     landed(fs.at[oc], f_s.at[0])
 
     def drain(j):
-        x_ring(j)[3]()
+        for r in range(2):
+            x_ring(j, r)[3]()
         landed(zr.at[j, pl.ds(1, ZY - 1)], z_s.at[j])
 
     for j in range(NB):
@@ -556,35 +560,44 @@
         z_ring(i)[3]()
         landed(xr.at[i, pl.ds(1, NX * NY - 1)], xo_s.at[i])
     landed(gcv, o_sem.at[4])
-    for copy in outs:
-        copy.wait()
-
-
-def deliver(*refs):
-    n = (len(refs) - 1) // 3
-    src, dst, held, sem = refs[:n], refs[n : 2 * n], refs[2 * n : 3 * n], refs[-1]
-    into = [pltpu.make_async_copy(s, h, sem.at[i]) for i, (s, h) in enumerate(zip(src, held))]
-    out = [pltpu.make_async_copy(h, d, sem.at[n + i]) for i, (h, d) in enumerate(zip(held, dst))]
+    landed(g_hbm.at[c], o_sem.at[1])
+    gain_out.wait()
+
+
+def deliver(
+    dims,
+    g_hbm, gg_hbm, gc_hbm, w_hbm, m1_hbm, m2_hbm,
+    nw_hbm, n1_hbm, n2_hbm, gg_out, gc_out,
+    gv, ggv, gcv, w16, m1v, m2v, nwv, n1v, n2v, sem,
+):
+    NZ, NY, NX, TH, H, D, NB, CB = dims
+    z, yl, x, c = (lax.axis_index(a) for a in DP)
+    row = pl.multiple_of(((z * NY + yl) * NX + x) * 16, 16)
+    pairs = [(gc_hbm, gcv), (gg_hbm, ggv), (g_hbm, gv), (w_hbm.at[pl.ds(row, 16), :], w16), (m1_hbm, m1v), (m2_hbm, m2v)]
+    into = [pltpu.make_async_copy(a, b, sem.at[i]) for i, (a, b) in enumerate(pairs)]
+    pairs = [(gcv, gc_out), (ggv, gg_out), (nwv, nw_hbm), (n1v, n1_hbm), (n2v, n2_hbm)]
+    out = [pltpu.make_async_copy(a, b, sem.at[6 + i]) for i, (a, b) in enumerate(pairs)]
     for copy in into:
         copy.start()
-    for first, second in zip(into, out):
-        first.wait()
-        second.start()
+    for i in range(2):
+        into[i].wait()
+        out[i].start()
+    for copy in into[2:]:
+        copy.wait()
+    for b in range(2 * NB):
+        cols = slice(b * CB, (b + 1) * CB)
+        g = gv[b // NB, b % NB]
+        first = beta_one * m1v[:, cols] + (1.0 - beta_one) * g
+        second = beta_two * m2v[:, cols] + (1.0 - beta_two) * g * g
+        both = w16[:, cols].astype(F32)
+        master = jnp.where(c == 0, both[:8], both[8:])
+        n1v[:, cols] = first
+        n2v[:, cols] = second
+        nwv[:, cols] = (master - learn_rate * first / (jnp.sqrt(second) + adam_floor)).astype(BF16)
+    for copy in out[2:]:
+        copy.start()
     for copy in out:
         copy.wait()
-
-
-def delivered(arrays):
-    space = pl.BlockSpec(memory_space=pl.ANY)
-    return pl.pallas_call(
-        deliver,
-        out_shape=[jax.ShapeDtypeStruct(a.shape, a.dtype) for a in arrays],
-        in_specs=[space] * len(arrays),
-        out_specs=[space] * len(arrays),
-        scratch_shapes=[pltpu.VMEM(a.shape, a.dtype) for a in arrays]
-        + [pltpu.SemaphoreType.DMA((2 * len(arrays),))],
-        name="deliver",
-    )(*arrays)
 
 
 def per_device(sizes, block, context, out_weight, cotangent, norm_gain, first_moment, second_moment):
@@ -600,9 +613,6 @@
     dims = (NZ, NY, NX, TH, H, D, NB, CB)
     dma = pltpu.SemaphoreType.DMA
     scratch = [
-        pltpu.VMEM((8, D), BF16),
-        pltpu.VMEM((8, D), F32),
-        pltpu.VMEM((8, D), F32),
         pltpu.VMEM((D,), F32),
         pltpu.VMEM((H // QR, 2, TH, QR), BF16),
         pltpu.VMEM((H // QR, TH, QR), F32),
@@ -621,18 +631,15 @@
         pltpu.VMEM((NB, 2, TH, CB), BF16),
         pltpu.VMEM((NB, NZ * NY * NX, 16, CB), F32),
         pltpu.VMEM((NB, max(ZY, NY * NX), 16, CB), F32),
-        pltpu.VMEM((NB, (NX - 1) * ZY, 16, CB), BF16),
+        pltpu.VMEM((NB, 2, (NX - 1) * NZ, 16, CB), BF16),
         pltpu.VMEM((NZB, (NZ - 1) * NY * NX, 16, CB), BF16),
-        pltpu.VMEM((NB, NX // 2, 2, ZY, 16, CB), BF16),
+        pltpu.VMEM((NB, 2, NX // 2, 2, NZ, 16, CB), BF16),
         pltpu.VMEM((NZB, NZ // 2, 2, NY * NX, 16, CB), BF16),
-        pltpu.VMEM((NB, NZ, NY, 16, CB), BF16),
+        pltpu.VMEM((NB, NY, NZ, 16, CB), BF16),
         pltpu.VMEM((NB, ZY, 16, CB), BF16),
         pltpu.VMEM((NZB, NY, NX, 16, CB), BF16),
         pltpu.VMEM((NZB, NX * NY, 16, CB), BF16),
         pltpu.VMEM((2, NB, 8, CB), F32),
-        pltpu.VMEM((2, NB, 8, CB), F32),
-        pltpu.VMEM((8, D), F32),
-        pltpu.VMEM((8, D), F32),
         pltpu.VMEM((NZ, rows8, CB), F32),
         pltpu.VMEM((NX, rows8, CB), F32),
         pltpu.VMEM((NY, rows8, CB), F32),
@@ -642,7 +649,7 @@
         dma((1,)), dma((NB2 + 1,)),
         dma((1,)), dma((NB,)),
         dma((1,)), dma((NB,)),
-        dma((NB,)), dma((NB, NX // 2)),
+        dma((NB, 2)), dma((NB, 2, NX // 2)),
         dma((NZB,)), dma((NZB, NZ // 2)),
         dma((NB,)), dma((NB,)),
         dma((NZB,)), dma((NZB,)),
@@ -653,24 +660,35 @@
     ]
     any_space = pl.BlockSpec(memory_space=pl.ANY)
     vmem = pl.BlockSpec(memory_space=pltpu.VMEM)
-    results = pl.pallas_call(
+    g, gg, gc = pl.pallas_call(
         functools.partial(kernel, dims),
         out_shape=[
-            jax.ShapeDtypeStruct((8, D), BF16),
-            jax.ShapeDtypeStruct((8, D), F32),
-            jax.ShapeDtypeStruct((8, D), F32),
+            jax.ShapeDtypeStruct((2, NB, 8, CB), F32),
             jax.ShapeDtypeStruct((D,), F32),
             jax.ShapeDtypeStruct((T, H), BF16),
         ],
-        in_specs=[any_space, any_space, any_space, vmem, any_space, any_space],
-        out_specs=[any_space] * 5,
+        in_specs=[any_space, any_space, any_space, vmem],
+        out_specs=[any_space] * 3,
         scratch_shapes=scratch,
         compiler_params=pltpu.CompilerParams(
             collective_id=0, has_side_effects=True, vmem_limit_bytes=60 * 1024 * 1024
         ),
         name="step",
-    )(context, out_weight, cotangent, norm_gain, first_moment[0], second_moment[0])
-    nw, n1, n2, gg, gc = delivered(results)
+    )(context, out_weight, cotangent, norm_gain)
+    shard = jax.ShapeDtypeStruct((8, D), F32)
+    results = [jax.ShapeDtypeStruct((8, D), BF16), shard, shard, jax.ShapeDtypeStruct((D,), F32)]
+    results.append(jax.ShapeDtypeStruct((T, H), BF16))
+    moved = [(2, NB, 8, CB), (D,), (T, H), (16, D), (8, D), (8, D), (8, D), (8, D), (8, D)]
+    types = [F32, F32, BF16, BF16, F32, F32, BF16, F32, F32]
+    nw, n1, n2, gg, gc = pl.pallas_call(
+        functools.partial(deliver, dims),
+        out_shape=results,
+        in_specs=[any_space] * 6,
+        out_specs=[any_space] * 5,
+        scratch_shapes=[pltpu.VMEM(a, b) for a, b in zip(moved, types)] + [dma((11,))],
+        compiler_params=pltpu.CompilerParams(vmem_limit_bytes=60 * 1024 * 1024),
+        name="deliver",
+    )(g, gg, gc, out_weight, first_moment[0], second_moment[0])
     return (nw[None], n1[None], n2[None], gg, gc)
 
 

time: 88.2 us -> 87.6 us (level)
  no operation moved by 1% of the time
where the time goes in v6:
time: 87.6 us; the launch traced here: 87.5 us
  Pallas kernels  86.9 us (99%)
    pallas_call x1, Pallas kernels, per_device(): pl.pallas_call(functools.partial(kernel, dims), out_shape=[jax.ShapeDtype...  84.7 us
    pallas_call x1, Pallas kernels, per_device(): pl.pallas_call(functools.partial(deliver, dims), out_shape=results, in_sp...  2.11 us

profile of v6, /device:TPU:1, one launch (start us, length us, event | category | flops | bytes accessed | tf_op | source)
XLA Modules:
  0.0 87.5 jit_solution(4648901643335802141)
XLA Ops:
  0.6 84.7 %step.1 = (f32[2,7,8,256]{3,2,1,0:T(8,128)}, f32[3584]{0:T(1024)}, bf16[320,1024]{1,0:T(8,128)(2,1)}) custom-call(bf16[320,1024]{1,0:T(8,128)(2,1)} %ctx_hbm.1, bf16[1024,3584]{1,0:T(8,128)(2,1)} %w_hbm.3, bf16[320,3584]{1,0:T(8,128)(2,1)} %cot_hbm.1, f32[3584]{0:T(1024)} %gain_ref.1), custom_call_target="tpu_custom_call" | custom-call | tf_op jit(solution)/shard_map/step/pallas_call | solution.py:663
  85.4 2.1 %deliver.1 = (bf16[8,3584]{1,0:T(8,128)(2,1)}, f32[8,3584]{1,0:T(8,128)}, f32[8,3584]{1,0:T(8,128)}, f32[3584]{0:T(1024)}, bf16[320,1024]{1,0:T(8,128)(2,1)}) custom-call(f32[2,7,8,256]{3,2,1,0:T(8,128)} %get-tuple-element.13.g_hbm, f32[3584]{0:T(1024)} %get-tuple-element.14.gg_hbm, bf16[320,1024]{1,0:T(8,128)(2,1)} %get-tuple-element.15.gc_hbm, ...), custom_call_target="tpu_custom_call" | custom-call | tf_op jit(solution)/shard_map/deliver/pallas_call | solution.py:683

commit v7 on v6

--- a/solution.py
+++ b/solution.py
@@ -534,9 +534,6 @@
 
     gain_out = pltpu.make_async_copy(gg_ref, gg_hbm, o_sem.at[0])
     gain_out.start()
-    with jax.named_scope("core_wait"):
-        landed(g_hbm.at[oc], f_r.at[0])
-
     ctx_swap().wait_send()
     landed(psend, p_s.at[0])
     for hop in hops:
@@ -560,6 +557,9 @@
         z_ring(i)[3]()
         landed(xr.at[i, pl.ds(1, NX * NY - 1)], xo_s.at[i])
     landed(gcv, o_sem.at[4])
+    with jax.named_scope("core_wait"):
+        landed(g_hbm.at[oc], f_r.at[0])
+
     landed(g_hbm.at[c], o_sem.at[1])
     gain_out.wait()
 

time: 87.6 us -> 87.6 us (level)
  no operation moved by 1% of the time
where the time goes in v7:
time: 87.6 us; the launch traced here: 87.4 us
  Pallas kernels  86.8 us (99%)
    pallas_call x1, Pallas kernels, per_device(): pl.pallas_call(functools.partial(kernel, dims), out_shape=[jax.ShapeDtype...  84.7 us
    pallas_call x1, Pallas kernels, per_device(): pl.pallas_call(functools.partial(deliver, dims), out_shape=results, in_sp...  2.11 us

profile of v7, /device:TPU:1, one launch (start us, length us, event | category | flops | bytes accessed | tf_op | source)
XLA Modules:
  0.0 87.4 jit_solution(8453512249960870035)
XLA Ops:
  0.6 84.7 %step.1 = (f32[2,7,8,256]{3,2,1,0:T(8,128)}, f32[3584]{0:T(1024)}, bf16[320,1024]{1,0:T(8,128)(2,1)}) custom-call(bf16[320,1024]{1,0:T(8,128)(2,1)} %ctx_hbm.1, bf16[1024,3584]{1,0:T(8,128)(2,1)} %w_hbm.3, bf16[320,3584]{1,0:T(8,128)(2,1)} %cot_hbm.1, f32[3584]{0:T(1024)} %gain_ref.1), custom_call_target="tpu_custom_call" | custom-call | tf_op jit(solution)/shard_map/step/pallas_call | solution.py:663
  85.3 2.1 %deliver.1 = (bf16[8,3584]{1,0:T(8,128)(2,1)}, f32[8,3584]{1,0:T(8,128)}, f32[8,3584]{1,0:T(8,128)}, f32[3584]{0:T(1024)}, bf16[320,1024]{1,0:T(8,128)(2,1)}) custom-call(f32[2,7,8,256]{3,2,1,0:T(8,128)} %get-tuple-element.13.g_hbm, f32[3584]{0:T(1024)} %get-tuple-element.14.gg_hbm, bf16[320,1024]{1,0:T(8,128)(2,1)} %get-tuple-element.15.gc_hbm, ...), custom_call_target="tpu_custom_call" | custom-call | tf_op jit(solution)/shard_map/deliver/pallas_call | solution.py:683
